TPU v7x, 32 devices: a whole 2x2x4 slice. The times are simulated.
32 devices in a mesh: dp: 2 (over y), ep: 16 (over z, x, core).
Axes of the slice: x: 2, y: 2, z: 4, core: 2. Of those that a mesh axis runs over, the one named last changes fastest.
Arguments:
- tokens: bfloat16 [16, 2, 1, 3584], P('ep', 'dp'), may hold values from -6 to 6
- gate_weights: bfloat16 [16, 2, 1, 8], P('ep', 'dp'), may hold values from 0.099609375 to 0.59765625
- expert_ids: int32 [16, 2, 1, 8], P('ep', 'dp'), may hold values from 0 to 15, all different within a row; in each aligned block of 2 rows (0 to 1, 2 to 3, ..., all dimensions but the last counted through in order) at most 2 rows name the same one
- gate_proj: bfloat16 [16, 3584, 2048], P('ep', None, 'dp'), may hold values from -0.09375 to 0.09375
- up_proj: bfloat16 [16, 3584, 2048], P('ep', None, 'dp'), may hold values from -0.09375 to 0.09375
- down_proj: bfloat16 [16, 2048, 3584], P('ep', 'dp'), may hold values from -0.125 to 0.125
Outputs:
- mixed: bfloat16 [16, 2, 1, 3584], P('ep', 'dp')
Inputs may be any that keep to these rules, and one draw needn't show every extreme that they name: `expert_ids`: each token names 8 different experts. Among the 2 tokens of one index of the first dimension, no expert is named more than 2 times, a bound that some block reaches.
All inputs are finite; a program needn't handle non-finite values.
Results may differ from a plain program's by a relative error of at most 0.02.
Values may be sent and summed in bfloat16 or wider, within the bound.
No kernel may reach another device: no remote copies, remote signals or barrier semaphores. Data moves between devices by JAX's collectives and lax.ppermute only.
A program may use at most 64 MiB of HBM per device.

v0:
```python
import jax
import jax.numpy as jnp
from jax import lax
from jax.sharding import PartitionSpec as P


def placing(flat_ids, expert_count, capacity):
    labels = jnp.arange(expert_count, dtype=jnp.int32)
    onehot = (flat_ids[:, None] == labels[None, :]).astype(jnp.int32)
    earlier = jnp.cumsum(onehot, axis=0) - onehot
    slot_index = jnp.sum(earlier * onehot, axis=1)
    destination = flat_ids * capacity + slot_index
    targets = jnp.arange(expert_count * capacity, dtype=jnp.int32)
    return (destination[:, None] == targets[None, :]).astype(jnp.float32)


def body(tokens, gate_weights, expert_ids, gate_proj, up_proj, down_proj):
    group_count = lax.axis_size("dp")
    expert_count = lax.axis_size("ep")
    token_count = tokens.shape[2]
    feature_count = tokens.shape[3]
    top_count = expert_ids.shape[3]
    capacity = min(
        group_count * token_count, token_count * (group_count * top_count // expert_count + 1)
    )
    token_total = group_count * token_count
    slot_total = expert_count * capacity
    column_count = feature_count // group_count
    all_ids = lax.all_gather(expert_ids, "dp", axis=1, tiled=True)
    placed = placing(all_ids.reshape(-1), expert_count, capacity)
    selection = jnp.sum(placed.reshape(token_total, top_count, slot_total), axis=1)
    selection_t = selection.T.astype(jnp.bfloat16)
    token_rows, all_weights = (
        lax.all_gather(tokens, "dp", axis=1, tiled=True),
        lax.all_gather(gate_weights, "dp", axis=1, tiled=True),
    )
    buffer = jnp.dot(
        selection_t,
        token_rows.reshape(token_total, feature_count),
        preferred_element_type=jnp.float32,
    ).astype(jnp.bfloat16)
    received = lax.all_to_all(
        buffer.reshape(expert_count, capacity, feature_count),
        "ep",
        split_axis=0,
        concat_axis=0,
        tiled=True,
    )
    slot_rows = received.reshape(slot_total, feature_count)
    gate_act = jnp.dot(slot_rows, gate_proj[0], preferred_element_type=jnp.float32)
    up_act = jnp.dot(slot_rows, up_proj[0], preferred_element_type=jnp.float32)
    hidden = (jax.nn.silu(gate_act) * up_act).astype(jnp.bfloat16)
    down_mat = down_proj[0]
    summed_t = lax.psum_scatter(
        lax.dot_general(
            down_mat, hidden, (((0,), (1,)), ((), ())), preferred_element_type=jnp.float32
        ).astype(jnp.bfloat16),
        "dp",
        scatter_dimension=0,
        tiled=True,
    ).astype(jnp.float32)
    summed = summed_t.T.astype(jnp.bfloat16).reshape(expert_count, capacity, column_count)
    returned = lax.all_to_all(summed, "ep", split_axis=0, concat_axis=0, tiled=True)
    weight_flat = all_weights.reshape(-1).astype(jnp.float32)
    weighted = jnp.sum(
        (placed * weight_flat[:, None]).reshape(token_total, top_count, slot_total), axis=1
    )
    mixed = jnp.dot(
        weighted,
        returned.reshape(slot_total, column_count).astype(jnp.float32),
        precision=lax.Precision.HIGHEST,
    ).astype(jnp.bfloat16)
    own = lax.all_to_all(
        mixed.reshape(group_count, token_count, column_count),
        "dp",
        split_axis=0,
        concat_axis=2,
        tiled=True,
    )
    return own.reshape(1, 1, token_count, feature_count)


def solution(mesh):
    placed = (
        P("ep", "dp", None, None),
        P("ep", "dp", None, None),
        P("ep", "dp", None, None),
        P("ep", None, "dp"),
        P("ep", None, "dp"),
        P("ep", "dp", None),
    )
    return jax.shard_map(
        body, mesh=mesh, in_specs=placed, out_specs=P("ep", "dp", None, None), check_vma=False
    )
```

profile of v0, /device:TPU:0, one launch (start us, length us, event | category | flops | bytes accessed | tf_op | source)
XLA Modules:
  0.0 90.4 jit_solution(14572636809706801968)
XLA Ops:
  6.5 0.0 reduce-scatter.2.cloned.1.call-start
  6.5 5.4 %all_gather.9 = s32[1,2,1,8]{3,2,0,1:T(1,128)S(1)} all-gather(s32[1,1,1,8]{3,2,0,1:T(1,128)} %bitcast.43), channel_id=1, replica_groups=mesh['dp'=2,'ep'=16] {'dp'}, dimensions={1}, use_global_device_ids=true | all-gather | bytes 96 | tf_op jit(solution)/shard_map/all_gather | solution.py:29
  11.9 0.5 broadcast.39
  12.4 0.7 fusion.32
  13.1 0.1 eq.30
  13.2 0.1 fusion.29
  13.3 0.2 select_reduce_fusion.1
  13.5 0.1 reduce_sum.30
  13.6 4.4 %all_gather.10 = bf16[1,2,1,8]{3,2,0,1:T(2,128)(2,1)S(1)} all-gather(bf16[1,1,1,8]{3,2,0,1:T(2,128)(2,1)} %bitcast.44), channel_id=1, replica_groups=mesh['dp'=2,'ep'=16] {'dp'}, dimensions={1}, use_global_device_ids=true | all-gather | bytes 48 | tf_op jit(solution)/shard_map/all_gather | solution.py:35
  17.9 4.6 %all_gather.11 = bf16[1,2,1,3584]{3,2,0,1:T(2,128)(2,1)S(1)} all-gather(bf16[1,1,1,3584]{3,2,0,1:T(2,128)(2,1)} %bitcast.40), channel_id=1, replica_groups=mesh['dp'=2,'ep'=16] {'dp'}, dimensions={1}, use_global_device_ids=true | all-gather | bytes 21504 | tf_op jit(solution)/shard_map/all_gather | solution.py:34
  22.6 0.1 convert_reduce_fusion
  22.6 0.3 convolution_convert_fusion
  22.9 0.1 reshape.70
  23.0 15.6 %all_to_all.19 = bf16[16,2,3584]{2,1,0:T(2,128)(2,1)S(1)} all-to-all(bf16[16,2,3584]{2,1,0:T(2,128)(2,1)S(1)} %reshape.70), channel_id=1, replica_groups=mesh['dp'=2,'ep'=16] {'ep'}, dimensions={0} | all-to-all | bytes 458752 | tf_op jit(solution)/shard_map/all_to_all | solution.py:42
  38.7 0.1 reshape.71
  38.7 4.4 %fusion.4 = f32[32,1024]{1,0:T(8,128)S(1)} fusion(bf16[32,3584]{1,0:T(8,128)(2,1)S(1)} %reshape.71, bf16[1,3584,1024]{2,1,0:T(8,128)(2,1)} %param.9), kind=kOutput, calls=%fused_computation.4 | convolution fusion | flops 234881024 | bytes 7700480 | tf_op jit(solution)/shard_map/dot_general | solution.py:50
  43.2 8.5 %fusion.9 = bf16[3584,32]{0,1:T(8,128)(2,1)} fusion(bf16[1,1024,3584]{2,1,0:T(8,128)(2,1)} %param.11, bf16[32,3584]{1,0:T(8,128)(2,1)S(1)} %reshape.71, bf16[1,3584,1024]{2,1,0:T(8,128)(2,1)} %param.10, f32[32,1024]{1,0:T(8,128)S(1)} %fusion.4), kind=kOutput, calls=%fused_computation.8 | convolution fusion | flops 470073344 | bytes 15269888 | tf_op jit(solution)/shard_map/dot_general | solution.py:55
  51.7 0.0 reduce-scatter.2.cloned.1.call-update
  51.7 9.6 %reduce-scatter.2.cloned.1.call-done = bf16[1792,32]{0,1:T(8,128)(2,1)} async-done(((bf16[3584,32]{0,1:T(8,128)(2,1)}), bf16[1792,32]{0,1:T(8,128)(2,1)}) %reduce-scatter.2.cloned.1.call-update) | async-done | bytes 114704 | tf_op jit(solution)/shard_map/reduce_scatter | solution.py:54
  61.3 0.9 %reshape.72 = bf16[16,2,1792]{2,1,0:T(2,128)(2,1)S(1)} reshape(bf16[32,1792]{1,0:T(8,128)(2,1)} %bitcast.39) | data formatting | bytes 229376 | tf_op jit(solution)/shard_map/reshape | solution.py:62
  62.3 13.0 %all_to_all.20 = bf16[16,2,1792]{2,1,0:T(2,128)(2,1)S(1)} all-to-all(bf16[16,2,1792]{2,1,0:T(2,128)(2,1)S(1)} %reshape.72), channel_id=1, replica_groups=mesh['dp'=2,'ep'=16] {'ep'}, dimensions={0} | all-to-all | bytes 229376 | tf_op jit(solution)/shard_map/all_to_all | solution.py:63
  75.4 0.2 fusion.12
  75.6 0.5 broadcast.40
  76.1 0.7 reduce.5
  76.8 6.1 %all_to_all.21 = bf16[2,2,896]{2,1,0:T(2,128)(2,1)S(1)} all-to-all(bf16[2,2,896]{2,1,0:T(2,128)(2,1)S(1)} %reshape.86), channel_id=1, replica_groups=mesh['dp'=2,'ep'=16] {'dp'}, dimensions={0} | all-to-all | bytes 14336 | tf_op jit(solution)/shard_map/all_to_all | solution.py:73
  82.9 0.6 reshape.87
  (5 shorter events, 0.1 us)
Async XLA Ops:
  6.5 54.8 %reduce-scatter.2.cloned.1.call-start = ((), (), s32[]{:S(2)}) async-start(), calls=%async_computation.4 | async-start | bytes 344064 | tf_op jit(solution)/shard_map/reduce_scatter | solution.py:54
Sparse Core Ops, SparseCore 0:
  51.8 9.4 reduce-scatter.1
where the time goes:
time: 90.7 us; the launch traced here: 90.4 us
  blocking collectives  49.2 us (54%)
  matrix products  13.4 us (15%)
  between operations  13.4 us (15%)
  waiting for transfers between devices  9.65 us (11%)
  local copies, waits for them, and re-layouts  3 us (3%)
  other arithmetic  1.72 us (2%)
    all_to_all x1, blocking collectives, body(): lax.all_to_all(buffer.reshape(expert_count, capacity, feature_count), 'ep...  15.6 us
    all_to_all x1, blocking collectives, body(): lax.all_to_all(summed, 'ep', split_axis=0, concat_axis=0, tiled=True)  13 us
    reduce_scatter x1, waiting for transfers between devices, body(): lax.psum_scatter(lax.dot_general(down_mat, hidden, (((0,), (1,)), ((), ()...  9.63 us
    dot_general x1, matrix products, body(): lax.dot_general(down_mat, hidden, (((0,), (1,)), ((), ())), preferred_ele...  8.5 us
    all_to_all x1, blocking collectives, body(): lax.all_to_all(mixed.reshape(group_count, token_count, column_count), 'dp...  6.14 us
    all_gather x1, blocking collectives, body(): all_ids = lax.all_gather(expert_ids, 'dp', axis=1, tiled=True)  5.38 us
    all_gather x1, blocking collectives, body(): lax.all_gather(tokens, 'dp', axis=1, tiled=True)  4.61 us
    dot_general x1, matrix products, body(): jnp.dot(slot_rows, gate_proj[0], preferred_element_type=jnp.float32)  4.45 us
  transfers between devices with their start and end apart: 1, of which 1 were waited for; matrix products, arithmetic and copies ran while one was open for 0% of the time, Pallas kernels for 0%

commit v1 on v0

v1 whole, which is shorter than its diff:
```python
import functools

import jax
import jax.numpy as jnp
from jax import lax
from jax.experimental import pallas as pl
from jax.experimental.pallas import tpu as pltpu
from jax.sharding import PartitionSpec as P

VMEM = pl.BlockSpec(memory_space=pltpu.VMEM)


def prepare_kernel(experts, tokens_ref, weights_ref, ids_ref, sent_ref, mix_ref):
    devices, _, half = sent_ref.shape
    row = tokens_ref[...].astype(jnp.float32)
    pair = jnp.concatenate([row[:, :half], row[:, half:]], axis=0).astype(jnp.bfloat16)

    @pl.loop(0, devices)
    def _(i):
        sent_ref[i] = pair

    shape = mix_ref.shape
    column = lax.broadcasted_iota(jnp.int32, shape, 1)
    expert = lax.rem(lax.div(column, 2), experts)
    mix = jnp.zeros(shape, jnp.float32)
    for k in range(ids_ref.shape[1]):
        weight = weights_ref[:, k : k + 1].astype(jnp.float32)
        mix = mix + jnp.where(expert == ids_ref[:, k : k + 1], weight, 0.0)
    own = lax.broadcasted_iota(jnp.int32, shape, 0) == lax.rem(column, 2)
    mix_ref[...] = jnp.where(own, mix, 0.0).astype(jnp.bfloat16)


def ffn_kernel(x_ref, gate_ref, up_ref, down_ref, out_ref, hidden_ref):
    devices, _, half = x_ref.shape
    width = gate_ref.shape[1]
    step = min(256, width)
    rows = x_ref[...].reshape(2 * devices, half)
    even = lax.rem(lax.broadcasted_iota(jnp.int32, (2 * devices, step), 0), 2) == 0

    def project(ref, columns):
        low = jnp.dot(rows, ref[:half, columns], preferred_element_type=jnp.float32)
        high = jnp.dot(rows, ref[half:, columns], preferred_element_type=jnp.float32)
        return jnp.where(
            even, low + pltpu.roll(high, 2 * devices - 1, 0), high + pltpu.roll(low, 1, 0)
        )

    @pl.loop(0, width // step)
    def _(i):
        columns = pl.ds(pl.multiple_of(i * step, step), step)
        gate, up = project(gate_ref, columns), project(up_ref, columns)
        hidden_ref[:, columns] = (gate / (1.0 + jnp.exp(-gate)) * up).astype(jnp.bfloat16)

    hidden = hidden_ref[...]
    out_step = 256 if half % 256 == 0 else 128
    even_out = lax.rem(lax.broadcasted_iota(jnp.int32, (2 * devices, out_step), 0), 2) == 0

    @pl.loop(0, half // out_step)
    def _(i):
        start = pl.multiple_of(i * out_step, out_step)
        low = jnp.dot(hidden, down_ref[:, pl.ds(start, out_step)], preferred_element_type=jnp.float32)
        high = jnp.dot(
            hidden, down_ref[:, pl.ds(start + half, out_step)], preferred_element_type=jnp.float32
        )
        out = jnp.where(even_out, low, high).astype(jnp.bfloat16)
        out_ref[:, :, pl.ds(start, out_step)] = out.reshape(devices, 2, out_step)


def mix_kernel(mix_ref, parts_ref, out_ref):
    devices, _, half = parts_ref.shape
    rows = parts_ref[...].reshape(2 * devices, half)
    mixed = jnp.dot(mix_ref[...], rows, preferred_element_type=jnp.float32)
    out_ref[:, :half] = mixed[0:1].astype(jnp.bfloat16)
    out_ref[:, half:] = mixed[1:2].astype(jnp.bfloat16)


def body(tokens, gate_weights, expert_ids, gate_proj, up_proj, down_proj):
    groups, experts = lax.axis_size("dp"), lax.axis_size("ep")
    devices = groups * experts
    axes = ("dp", "ep")
    features, width = tokens.shape[3], gate_proj.shape[2]
    half = features // 2
    sent, mix = pl.pallas_call(
        functools.partial(prepare_kernel, experts),
        out_shape=(
            jax.ShapeDtypeStruct((devices, 2, half), jnp.bfloat16),
            jax.ShapeDtypeStruct((16, 2 * devices), jnp.bfloat16),
        ),
        in_specs=[VMEM] * 3,
        out_specs=(VMEM, VMEM),
        compiler_params=pltpu.CompilerParams(vmem_limit_bytes=24 << 20),
        name="prepare",
    )(tokens[0, 0], gate_weights[0, 0], expert_ids[0, 0])
    rows = lax.all_to_all(sent, axes, 0, 0, tiled=True)
    gate, up, down = (
        pltpu.with_memory_space_constraint(w[0], pltpu.VMEM) for w in (gate_proj, up_proj, down_proj)
    )
    out = pl.pallas_call(
        ffn_kernel,
        out_shape=jax.ShapeDtypeStruct((devices, 2, half), jnp.bfloat16),
        in_specs=[VMEM] * 4,
        out_specs=VMEM,
        scratch_shapes=[pltpu.VMEM((2 * devices, width), jnp.bfloat16)],
        compiler_params=pltpu.CompilerParams(vmem_limit_bytes=24 << 20),
        cost_estimate=pl.CostEstimate(
            flops=12 * devices * features * width,
            bytes_accessed=6 * features * width,
            transcendentals=2 * devices * width,
        ),
        name="ffn",
    )(rows, gate, up, down)
    parts = lax.all_to_all(out, axes, 0, 0, tiled=True)
    mixed = pl.pallas_call(
        mix_kernel,
        out_shape=jax.ShapeDtypeStruct((1, features), jnp.bfloat16),
        in_specs=[VMEM] * 2,
        out_specs=VMEM,
        compiler_params=pltpu.CompilerParams(vmem_limit_bytes=24 << 20),
        name="mix",
    )(mix, parts)
    return mixed[None, None]


def solution(mesh):
    placed = (
        P("ep", "dp", None, None),
        P("ep", "dp", None, None),
        P("ep", "dp", None, None),
        P("ep", None, "dp"),
        P("ep", None, "dp"),
        P("ep", "dp", None),
    )
    return jax.shard_map(
        body, mesh=mesh, in_specs=placed, out_specs=P("ep", "dp", None, None), check_vma=False
    )
```

time: 90.7 us -> 46.7 us (0.51)
  blocking collectives: 49.2 us -> 28.6 us
  matrix products: 13.4 us -> 0 us
  between operations: 13.4 us -> 0.02 us
  waiting for transfers between devices: 9.65 us -> 0 us
  local copies, waits for them, and re-layouts: 3 us -> 11.3 us
  Pallas kernels: 0 us -> 6.5 us
  other arithmetic: 1.72 us -> 0 us
    all_gather x3 -> x0, blocking collectives: 14.4 us -> none  [the longest x1 5.38 us: body(): all_ids = lax.all_gather(expert_ids, 'dp', axis=1, tiled=True)]
    dot_general x4 -> x0, matrix products: 13.4 us -> none  [the longest x1 8.5 us: body(): lax.dot_general(down_mat, hidden, (((0,), (1,)), ((), ())), preferred_ele...]
    unnamed x2 -> x12, local copies, waits for them, and re-layouts: 0.65 us -> 11.3 us
    reduce_scatter x1 -> x0, waiting for transfers between devices: 9.63 us -> none  [body(): lax.psum_scatter(lax.dot_general(down_mat, hidden, (((0,), (1,)), ((), ()...]
    pallas_call x0 -> x3, Pallas kernels: none -> 6.5 us  [the longest x1 5.32 us: body(): pl.pallas_call(ffn_kernel, out_shape=jax.ShapeDtypeStruct((devices, 2, ha...]
    all_to_all x3 -> x2, blocking collectives: 34.8 us -> 28.6 us  [the longest x1 16.7 us: body(): rows = lax.all_to_all(sent, axes, 0, 0, tiled=True)]
    reshape x5 -> x0, local copies, waits for them, and re-layouts: 1.68 us -> none  [the longest x1 0.94 us: body(): summed_t.T.astype(jnp.bfloat16)]
  transfers between devices with their start and end apart: 1 -> 0, of which waited for: 1 -> 0; matrix products, arithmetic and copies ran while one was open for 0% -> 0% of each run, Pallas kernels for 0% -> 0%
where the time goes in v1:
time: 46.7 us; the launch traced here: 46.4 us
  blocking collectives  28.6 us (61%)
  local copies, waits for them, and re-layouts  11.3 us (24%)
  Pallas kernels  6.5 us (14%)
    all_to_all x1, blocking collectives, body(): rows = lax.all_to_all(sent, axes, 0, 0, tiled=True)  16.7 us
    all_to_all x1, blocking collectives, body(): parts = lax.all_to_all(out, axes, 0, 0, tiled=True)  11.9 us
    unnamed x12, local copies, waits for them, and re-layouts  11.3 us
    pallas_call x1, Pallas kernels, body(): pl.pallas_call(ffn_kernel, out_shape=jax.ShapeDtypeStruct((devices, 2, ha...  5.32 us

profile of v1, /device:TPU:0, one launch (start us, length us, event | category | flops | bytes accessed | tf_op | source)
XLA Modules:
  0.0 46.4 jit_solution(7817073929390065270)
XLA Ops:
  0.0 0.0 copy-start.3
  0.0 0.7 %copy-done.3 = bf16[1,1,1,3584]{3,2,1,0:T(2,128)(2,1)S(1)} copy-done((bf16[1,1,1,3584]{3,2,1,0:T(2,128)(2,1)S(1)}, bf16[1,1,1,3584]{3,2,1,0:T(2,128)(2,1)}, u32[]{:S(2)}) %copy-start.3) | copy-done | bytes 7192
  0.7 0.0 copy-start.4
  0.7 0.7 %copy-done.4 = bf16[1,1,1,8]{3,2,1,0:T(2,128)(2,1)S(1)} copy-done((bf16[1,1,1,8]{3,2,1,0:T(2,128)(2,1)S(1)}, bf16[1,1,1,8]{3,2,1,0:T(2,128)(2,1)}, u32[]{:S(2)}) %copy-start.4) | copy-done | bytes 40
  1.4 0.0 copy-start.5
  1.4 0.7 %copy-done.5 = s32[1,1,1,8]{3,2,1,0:T(1,128)S(1)} copy-done((s32[1,1,1,8]{3,2,1,0:T(1,128)S(1)}, s32[1,1,1,8]{3,2,1,0:T(1,128)}, u32[]{:S(2)}) %copy-start.5) | copy-done | bytes 56
  2.0 0.4 prepare.1
  2.4 16.7 %all_to_all.10.x_ref = bf16[32,2,1792]{2,1,0:T(2,128)(2,1)S(1)} all-to-all(bf16[32,2,1792]{2,1,0:T(2,128)(2,1)S(1)} %get-tuple-element.8), channel_id=1, replica_groups=mesh['dp'=2,'ep'=16] {'dp','ep'}, dimensions={0} | all-to-all | bytes 458752 | tf_op jit(solution)/shard_map/all_to_all | solution.py:93
  19.1 0.0 copy-start
  19.1 3.1 %copy-done = bf16[1,3584,1024]{2,1,0:T(8,128)(2,1)S(1)} copy-done((bf16[1,3584,1024]{2,1,0:T(8,128)(2,1)S(1)}, bf16[1,3584,1024]{2,1,0:T(8,128)(2,1)}, u32[]{:S(2)}) %copy-start) | copy-done | bytes 7340056
  22.2 0.0 copy-start.1
  22.2 3.1 %copy-done.1 = bf16[1,3584,1024]{2,1,0:T(8,128)(2,1)S(1)} copy-done((bf16[1,3584,1024]{2,1,0:T(8,128)(2,1)S(1)}, bf16[1,3584,1024]{2,1,0:T(8,128)(2,1)}, u32[]{:S(2)}) %copy-start.1) | copy-done | bytes 7340056
  25.3 0.0 copy-start.2
  25.3 3.1 %copy-done.2 = bf16[1,1024,3584]{2,1,0:T(8,128)(2,1)S(1)} copy-done((bf16[1,1024,3584]{2,1,0:T(8,128)(2,1)S(1)}, bf16[1,1024,3584]{2,1,0:T(8,128)(2,1)}, u32[]{:S(2)}) %copy-start.2) | copy-done | bytes 7340056
  28.4 5.3 %ffn.1 = bf16[32,2,1792]{2,1,0:T(2,128)(2,1)S(1)} custom-call(bf16[32,2,1792]{2,1,0:T(2,128)(2,1)S(1)} %all_to_all.10.x_ref, bf16[3584,1024]{1,0:T(8,128)(2,1)S(1)} %bitcast.7, bf16[3584,1024]{1,0:T(8,128)(2,1)S(1)} %bitcast.8, bf16[1024,3584]{1,0:T(8,128)(2,1)S(1)} %bitcast.9), custom_call_target="tpu_custom_call" | custom-call | flops 1409286144 | bytes 22020096 | tf_op jit(solution)/shard_map/ffn/pallas_call | solution.py:97
  33.7 11.9 %all_to_all.11.parts_ref = bf16[32,2,1792]{2,1,0:T(2,128)(2,1)S(1)} all-to-all(bf16[32,2,1792]{2,1,0:T(2,128)(2,1)S(1)} %ffn.1), channel_id=1, replica_groups=mesh['dp'=2,'ep'=16] {'dp','ep'}, dimensions={0} | all-to-all | bytes 458752 | tf_op jit(solution)/shard_map/all_to_all | solution.py:111
  45.7 0.8 %mix.1 = bf16[1,3584]{1,0:T(2,128)(2,1)} custom-call(bf16[16,64]{1,0:T(8,128)(2,1)S(1)} %get-tuple-element.7.mix_ref, bf16[32,2,1792]{2,1,0:T(2,128)(2,1)S(1)} %all_to_all.11.parts_ref), custom_call_target="tpu_custom_call" | custom-call | tf_op jit(solution)/shard_map/mix/pallas_call | solution.py:112
Async XLA Ops:
  0.0 0.7 %copy-start.3 = (bf16[1,1,1,3584]{3,2,1,0:T(2,128)(2,1)S(1)}, bf16[1,1,1,3584]{3,2,1,0:T(2,128)(2,1)}, u32[]{:S(2)}) copy-start(bf16[1,1,1,3584]{3,2,1,0:T(2,128)(2,1)} %param.6) | copy-start | bytes 21508
  0.7 0.7 %copy-start.4 = (bf16[1,1,1,8]{3,2,1,0:T(2,128)(2,1)S(1)}, bf16[1,1,1,8]{3,2,1,0:T(2,128)(2,1)}, u32[]{:S(2)}) copy-start(bf16[1,1,1,8]{3,2,1,0:T(2,128)(2,1)} %param.7) | copy-start | bytes 52
  1.4 0.7 %copy-start.5 = (s32[1,1,1,8]{3,2,1,0:T(1,128)S(1)}, s32[1,1,1,8]{3,2,1,0:T(1,128)}, u32[]{:S(2)}) copy-start(s32[1,1,1,8]{3,2,1,0:T(1,128)} %param.8) | copy-start | bytes 100
  19.1 3.1 %copy-start = (bf16[1,3584,1024]{2,1,0:T(8,128)(2,1)S(1)}, bf16[1,3584,1024]{2,1,0:T(8,128)(2,1)}, u32[]{:S(2)}) copy-start(bf16[1,3584,1024]{2,1,0:T(8,128)(2,1)} %param.9) | copy-start | bytes 22020100
  22.2 3.1 %copy-start.1 = (bf16[1,3584,1024]{2,1,0:T(8,128)(2,1)S(1)}, bf16[1,3584,1024]{2,1,0:T(8,128)(2,1)}, u32[]{:S(2)}) copy-start(bf16[1,3584,1024]{2,1,0:T(8,128)(2,1)} %param.10) | copy-start | bytes 22020100
  25.3 3.1 %copy-start.2 = (bf16[1,1024,3584]{2,1,0:T(8,128)(2,1)S(1)}, bf16[1,1024,3584]{2,1,0:T(8,128)(2,1)}, u32[]{:S(2)}) copy-start(bf16[1,1024,3584]{2,1,0:T(8,128)(2,1)} %param.11) | copy-start | bytes 22020100

commit v2 on v1

--- a/solution.py
+++ b/solution.py
@@ -88,11 +88,12 @@
         in_specs=[VMEM] * 3,
         out_specs=(VMEM, VMEM),
         compiler_params=pltpu.CompilerParams(vmem_limit_bytes=24 << 20),
+        cost_estimate=pl.CostEstimate(flops=2 * 10**10, bytes_accessed=10**5, transcendentals=0),
         name="prepare",
     )(tokens[0, 0], gate_weights[0, 0], expert_ids[0, 0])
     rows = lax.all_to_all(sent, axes, 0, 0, tiled=True)
     gate, up, down = (
-        pltpu.with_memory_space_constraint(w[0], pltpu.VMEM) for w in (gate_proj, up_proj, down_proj)
+        w[0] for w in (gate_proj, up_proj, down_proj)
     )
     out = pl.pallas_call(
         ffn_kernel,

time: 46.7 us -> 37.5 us (0.80)
  local copies, waits for them, and re-layouts: 11.3 us -> 2.03 us
    unnamed x12, local copies, waits for them, and re-layouts: 11.3 us -> 2.03 us
where the time goes in v2:
time: 37.5 us; the launch traced here: 37.2 us
  blocking collectives  28.6 us (76%)
  Pallas kernels  6.51 us (17%)
  local copies, waits for them, and re-layouts  2.03 us (5%)
    all_to_all x1, blocking collectives, body(): rows = lax.all_to_all(sent, axes, 0, 0, tiled=True)  16.7 us
    all_to_all x1, blocking collectives, body(): parts = lax.all_to_all(out, axes, 0, 0, tiled=True)  11.9 us
    pallas_call x1, Pallas kernels, body(): pl.pallas_call(ffn_kernel, out_shape=jax.ShapeDtypeStruct((devices, 2, ha...  5.32 us
    unnamed x12, local copies, waits for them, and re-layouts  2.03 us
    pallas_call x1, Pallas kernels, body(): pl.pallas_call(mix_kernel, out_shape=jax.ShapeDtypeStruct((1, features),...  0.77 us

profile of v2, /device:TPU:0, one launch (start us, length us, event | category | flops | bytes accessed | tf_op | source)
XLA Modules:
  0.0 37.2 jit_solution(3958930324759018593)
XLA Ops:
  0.0 0.0 copy-start.3
  0.0 0.7 %copy-done.3 = bf16[1,1,1,3584]{3,2,1,0:T(2,128)(2,1)S(1)} copy-done((bf16[1,1,1,3584]{3,2,1,0:T(2,128)(2,1)S(1)}, bf16[1,1,1,3584]{3,2,1,0:T(2,128)(2,1)}, u32[]{:S(2)}) %copy-start.3) | copy-done | bytes 7192
  0.7 0.0 copy-start.4
  0.7 0.7 %copy-done.4 = bf16[1,1,1,8]{3,2,1,0:T(2,128)(2,1)S(1)} copy-done((bf16[1,1,1,8]{3,2,1,0:T(2,128)(2,1)S(1)}, bf16[1,1,1,8]{3,2,1,0:T(2,128)(2,1)}, u32[]{:S(2)}) %copy-start.4) | copy-done | bytes 40
  1.4 0.0 copy-start.5
  1.4 0.7 %copy-done.5 = s32[1,1,1,8]{3,2,1,0:T(1,128)S(1)} copy-done((s32[1,1,1,8]{3,2,1,0:T(1,128)S(1)}, s32[1,1,1,8]{3,2,1,0:T(1,128)}, u32[]{:S(2)}) %copy-start.5) | copy-done | bytes 56
  2.0 0.0 copy-start
  2.0 0.0 copy-start.1
  2.0 0.0 copy-start.2
  2.0 0.4 %prepare.1 = (bf16[32,2,1792]{2,1,0:T(2,128)(2,1)S(1)}, bf16[16,64]{1,0:T(8,128)(2,1)S(1)}) custom-call(bf16[1,3584]{1,0:T(2,128)(2,1)S(1)} %bitcast.10, bf16[1,8]{1,0:T(2,128)(2,1)S(1)} %bitcast.11, s32[1,8]{1,0:T(1,128)S(1)} %bitcast.12), custom_call_target="tpu_custom_call" | custom-call | flops 20000000000 | bytes 100000 | tf_op jit(solution)/shard_map/prepare/pallas_call | solution.py:82
  2.5 16.7 %all_to_all.10.x_ref = bf16[32,2,1792]{2,1,0:T(2,128)(2,1)S(1)} all-to-all(bf16[32,2,1792]{2,1,0:T(2,128)(2,1)S(1)} %get-tuple-element.8), channel_id=1, replica_groups=mesh['dp'=2,'ep'=16] {'dp','ep'}, dimensions={0} | all-to-all | bytes 458752 | tf_op jit(solution)/shard_map/all_to_all | solution.py:94
  19.2 0.0 copy-done
  19.2 0.0 copy-done.1
  19.2 0.0 copy-done.2
  19.2 5.3 %ffn.1 = bf16[32,2,1792]{2,1,0:T(2,128)(2,1)S(1)} custom-call(bf16[32,2,1792]{2,1,0:T(2,128)(2,1)S(1)} %all_to_all.10.x_ref, bf16[3584,1024]{1,0:T(8,128)(2,1)S(1)} %bitcast.7, bf16[3584,1024]{1,0:T(8,128)(2,1)S(1)} %bitcast.8, bf16[1024,3584]{1,0:T(8,128)(2,1)S(1)} %bitcast.9), custom_call_target="tpu_custom_call" | custom-call | flops 1409286144 | bytes 22020096 | tf_op jit(solution)/shard_map/ffn/pallas_call | solution.py:98
  24.5 11.9 %all_to_all.11.parts_ref = bf16[32,2,1792]{2,1,0:T(2,128)(2,1)S(1)} all-to-all(bf16[32,2,1792]{2,1,0:T(2,128)(2,1)S(1)} %ffn.1), channel_id=1, replica_groups=mesh['dp'=2,'ep'=16] {'dp','ep'}, dimensions={0} | all-to-all | bytes 458752 | tf_op jit(solution)/shard_map/all_to_all | solution.py:112
  36.4 0.8 %mix.1 = bf16[1,3584]{1,0:T(2,128)(2,1)} custom-call(bf16[16,64]{1,0:T(8,128)(2,1)S(1)} %get-tuple-element.7.mix_ref, bf16[32,2,1792]{2,1,0:T(2,128)(2,1)S(1)} %all_to_all.11.parts_ref), custom_call_target="tpu_custom_call" | custom-call | tf_op jit(solution)/shard_map/mix/pallas_call | solution.py:113
Async XLA Ops:
  0.0 0.7 %copy-start.3 = (bf16[1,1,1,3584]{3,2,1,0:T(2,128)(2,1)S(1)}, bf16[1,1,1,3584]{3,2,1,0:T(2,128)(2,1)}, u32[]{:S(2)}) copy-start(bf16[1,1,1,3584]{3,2,1,0:T(2,128)(2,1)} %param.6) | copy-start | bytes 21508
  0.7 0.7 %copy-start.4 = (bf16[1,1,1,8]{3,2,1,0:T(2,128)(2,1)S(1)}, bf16[1,1,1,8]{3,2,1,0:T(2,128)(2,1)}, u32[]{:S(2)}) copy-start(bf16[1,1,1,8]{3,2,1,0:T(2,128)(2,1)} %param.7) | copy-start | bytes 52
  1.4 0.7 %copy-start.5 = (s32[1,1,1,8]{3,2,1,0:T(1,128)S(1)}, s32[1,1,1,8]{3,2,1,0:T(1,128)}, u32[]{:S(2)}) copy-start(s32[1,1,1,8]{3,2,1,0:T(1,128)} %param.8) | copy-start | bytes 100
  2.0 17.1 %copy-start = (bf16[1,3584,1024]{2,1,0:T(8,128)(2,1)S(1)}, bf16[1,3584,1024]{2,1,0:T(8,128)(2,1)}, u32[]{:S(2)}) copy-start(bf16[1,3584,1024]{2,1,0:T(8,128)(2,1)} %param.9) | copy-start | bytes 22020100
  2.0 17.1 %copy-start.1 = (bf16[1,3584,1024]{2,1,0:T(8,128)(2,1)S(1)}, bf16[1,3584,1024]{2,1,0:T(8,128)(2,1)}, u32[]{:S(2)}) copy-start(bf16[1,3584,1024]{2,1,0:T(8,128)(2,1)} %param.10) | copy-start | bytes 22020100
  2.0 17.1 %copy-start.2 = (bf16[1,1024,3584]{2,1,0:T(8,128)(2,1)S(1)}, bf16[1,1024,3584]{2,1,0:T(8,128)(2,1)}, u32[]{:S(2)}) copy-start(bf16[1,1024,3584]{2,1,0:T(8,128)(2,1)} %param.11) | copy-start | bytes 22020100

commit v3 on v1

--- a/solution.py
+++ b/solution.py
@@ -7,10 +7,19 @@
 from jax.experimental.pallas import tpu as pltpu
 from jax.sharding import PartitionSpec as P
 
+LANES = 128
 VMEM = pl.BlockSpec(memory_space=pltpu.VMEM)
 
 
-def prepare_kernel(experts, tokens_ref, weights_ref, ids_ref, sent_ref, mix_ref):
+def block(total, rows):
+    return next(
+        size
+        for size in range(total, 0, -LANES)
+        if total % size == 0 and (size == LANES or rows * size <= 1 << 17)
+    )
+
+
+def prepare_kernel(tokens_ref, sent_ref):
     devices, _, half = sent_ref.shape
     row = tokens_ref[...].astype(jnp.float32)
     pair = jnp.concatenate([row[:, :half], row[:, half:]], axis=0).astype(jnp.bfloat16)
@@ -19,6 +28,8 @@
     def _(i):
         sent_ref[i] = pair
 
+
+def weigh(experts, weights_ref, ids_ref, mix_ref):
     shape = mix_ref.shape
     column = lax.broadcasted_iota(jnp.int32, shape, 1)
     expert = lax.rem(lax.div(column, 2), experts)
@@ -30,10 +41,13 @@
     mix_ref[...] = jnp.where(own, mix, 0.0).astype(jnp.bfloat16)
 
 
-def ffn_kernel(x_ref, gate_ref, up_ref, down_ref, out_ref, hidden_ref):
+def ffn_kernel(
+    experts, x_ref, gate_ref, up_ref, down_ref, weights_ref, ids_ref, out_ref, mix_ref, hidden_ref
+):
+    weigh(experts, weights_ref, ids_ref, mix_ref)
     devices, _, half = x_ref.shape
     width = gate_ref.shape[1]
-    step = min(256, width)
+    step = block(width, 2 * devices)
     rows = x_ref[...].reshape(2 * devices, half)
     even = lax.rem(lax.broadcasted_iota(jnp.int32, (2 * devices, step), 0), 2) == 0
 
@@ -51,7 +65,7 @@
         hidden_ref[:, columns] = (gate / (1.0 + jnp.exp(-gate)) * up).astype(jnp.bfloat16)
 
     hidden = hidden_ref[...]
-    out_step = 256 if half % 256 == 0 else 128
+    out_step = block(half, 2 * devices)
     even_out = lax.rem(lax.broadcasted_iota(jnp.int32, (2 * devices, out_step), 0), 2) == 0
 
     @pl.loop(0, half // out_step)
@@ -79,26 +93,25 @@
     axes = ("dp", "ep")
     features, width = tokens.shape[3], gate_proj.shape[2]
     half = features // 2
-    sent, mix = pl.pallas_call(
-        functools.partial(prepare_kernel, experts),
+    sent = pl.pallas_call(
+        prepare_kernel,
+        out_shape=jax.ShapeDtypeStruct((devices, 2, half), jnp.bfloat16),
+        in_specs=[VMEM],
+        out_specs=VMEM,
+        compiler_params=pltpu.CompilerParams(vmem_limit_bytes=24 << 20),
+        cost_estimate=pl.CostEstimate(flops=2 * 10**10, bytes_accessed=10**5, transcendentals=0),
+        name="prepare",
+    )(tokens[0, 0])
+    rows = lax.all_to_all(sent, axes, 0, 0, tiled=True)
+    gate, up, down = gate_proj[0], up_proj[0], down_proj[0]
+    out, mix = pl.pallas_call(
+        functools.partial(ffn_kernel, experts),
         out_shape=(
             jax.ShapeDtypeStruct((devices, 2, half), jnp.bfloat16),
             jax.ShapeDtypeStruct((16, 2 * devices), jnp.bfloat16),
         ),
-        in_specs=[VMEM] * 3,
+        in_specs=[VMEM] * 6,
         out_specs=(VMEM, VMEM),
-        compiler_params=pltpu.CompilerParams(vmem_limit_bytes=24 << 20),
-        name="prepare",
-    )(tokens[0, 0], gate_weights[0, 0], expert_ids[0, 0])
-    rows = lax.all_to_all(sent, axes, 0, 0, tiled=True)
-    gate, up, down = (
-        pltpu.with_memory_space_constraint(w[0], pltpu.VMEM) for w in (gate_proj, up_proj, down_proj)
-    )
-    out = pl.pallas_call(
-        ffn_kernel,
-        out_shape=jax.ShapeDtypeStruct((devices, 2, half), jnp.bfloat16),
-        in_specs=[VMEM] * 4,
-        out_specs=VMEM,
         scratch_shapes=[pltpu.VMEM((2 * devices, width), jnp.bfloat16)],
         compiler_params=pltpu.CompilerParams(vmem_limit_bytes=24 << 20),
         cost_estimate=pl.CostEstimate(
@@ -107,7 +120,7 @@
             transcendentals=2 * devices * width,
         ),
         name="ffn",
-    )(rows, gate, up, down)
+    )(rows, gate, up, down, gate_weights[0, 0], expert_ids[0, 0])
     parts = lax.all_to_all(out, axes, 0, 0, tiled=True)
     mixed = pl.pallas_call(
         mix_kernel,

time: 46.7 us -> 34.7 us (0.74)
  local copies, waits for them, and re-layouts: 11.3 us -> 0.73 us
  Pallas kernels: 6.5 us -> 5.07 us
    unnamed x12, local copies, waits for them, and re-layouts: 11.3 us -> 0.73 us
    pallas_call x2, Pallas kernels: 5.73 us -> 4.3 us  [the longest x1 4 us: body(): pl.pallas_call(functools.partial(ffn_kernel, experts), out_shape=(jax.Sha...]
where the time goes in v3:
time: 34.7 us; the launch traced here: 34.5 us
  blocking collectives  28.6 us (82%)
  Pallas kernels  5.07 us (15%)
  local copies, waits for them, and re-layouts  0.73 us (2%)
    all_to_all x1, blocking collectives, body(): rows = lax.all_to_all(sent, axes, 0, 0, tiled=True)  16.7 us
    all_to_all x1, blocking collectives, body(): parts = lax.all_to_all(out, axes, 0, 0, tiled=True)  11.9 us
    pallas_call x1, Pallas kernels, body(): pl.pallas_call(functools.partial(ffn_kernel, experts), out_shape=(jax.Sha...  4 us
    pallas_call x1, Pallas kernels, body(): pl.pallas_call(mix_kernel, out_shape=jax.ShapeDtypeStruct((1, features),...  0.77 us
    unnamed x12, local copies, waits for them, and re-layouts  0.73 us

profile of v3, /device:TPU:0, one launch (start us, length us, event | category | flops | bytes accessed | tf_op | source)
XLA Modules:
  0.0 34.5 jit_solution(13518925946212375573)
XLA Ops:
  0.0 0.0 copy-start.5
  0.0 0.7 %copy-done.5 = bf16[1,1,1,3584]{3,2,1,0:T(2,128)(2,1)S(1)} copy-done((bf16[1,1,1,3584]{3,2,1,0:T(2,128)(2,1)S(1)}, bf16[1,1,1,3584]{3,2,1,0:T(2,128)(2,1)}, u32[]{:S(2)}) %copy-start.5) | copy-done | bytes 7192
  0.7 0.0 copy-start
  0.7 0.0 copy-start.1
  0.7 0.0 copy-start.2
  0.7 0.0 copy-start.3
  0.7 0.0 copy-start.4
  0.7 0.3 prepare.1
  1.0 16.7 %all_to_all.10.x_ref = bf16[32,2,1792]{2,1,0:T(2,128)(2,1)S(1)} all-to-all(bf16[32,2,1792]{2,1,0:T(2,128)(2,1)S(1)} %prepare.1), channel_id=1, replica_groups=mesh['dp'=2,'ep'=16] {'dp','ep'}, dimensions={0} | all-to-all | bytes 458752 | tf_op jit(solution)/shard_map/all_to_all | solution.py:105
  17.7 0.0 copy-done
  17.7 0.0 copy-done.1
  17.7 0.0 copy-done.2
  17.7 0.0 copy-done.3
  17.8 0.0 copy-done.4
  17.8 4.0 %ffn.1 = (bf16[32,2,1792]{2,1,0:T(2,128)(2,1)S(1)}, bf16[16,64]{1,0:T(8,128)(2,1)S(1)}) custom-call(bf16[32,2,1792]{2,1,0:T(2,128)(2,1)S(1)} %all_to_all.10.x_ref, bf16[3584,1024]{1,0:T(8,128)(2,1)S(1)} %bitcast.7, bf16[3584,1024]{1,0:T(8,128)(2,1)S(1)} %bitcast.8, bf16[1024,3584]{1,0:T(8,128)(2,1)S(1)} %bitcast.9, bf16[1,8]{1,0:T(2,128)(2,1)S(1)} %bitcast.10, ...), custom_call_target="tpu_custom_call" | custom-call | flops 1409286144 | bytes 22020096 | tf_op jit(solution)/shard_map/ffn/pallas_call | solution.py:107
  21.8 11.9 %all_to_all.11.parts_ref = bf16[32,2,1792]{2,1,0:T(2,128)(2,1)S(1)} all-to-all(bf16[32,2,1792]{2,1,0:T(2,128)(2,1)S(1)} %get-tuple-element.8), channel_id=1, replica_groups=mesh['dp'=2,'ep'=16] {'dp','ep'}, dimensions={0} | all-to-all | bytes 458752 | tf_op jit(solution)/shard_map/all_to_all | solution.py:124
  33.7 0.8 %mix.1 = bf16[1,3584]{1,0:T(2,128)(2,1)} custom-call(bf16[16,64]{1,0:T(8,128)(2,1)S(1)} %get-tuple-element.7.mix_ref, bf16[32,2,1792]{2,1,0:T(2,128)(2,1)S(1)} %all_to_all.11.parts_ref), custom_call_target="tpu_custom_call" | custom-call | tf_op jit(solution)/shard_map/mix/pallas_call | solution.py:125
Async XLA Ops:
  0.0 0.7 %copy-start.5 = (bf16[1,1,1,3584]{3,2,1,0:T(2,128)(2,1)S(1)}, bf16[1,1,1,3584]{3,2,1,0:T(2,128)(2,1)}, u32[]{:S(2)}) copy-start(bf16[1,1,1,3584]{3,2,1,0:T(2,128)(2,1)} %param.6) | copy-start | bytes 21508
  0.7 17.0 %copy-start = (bf16[1,3584,1024]{2,1,0:T(8,128)(2,1)S(1)}, bf16[1,3584,1024]{2,1,0:T(8,128)(2,1)}, u32[]{:S(2)}) copy-start(bf16[1,3584,1024]{2,1,0:T(8,128)(2,1)} %param.9) | copy-start | bytes 22020100
  0.7 17.0 %copy-start.1 = (bf16[1,3584,1024]{2,1,0:T(8,128)(2,1)S(1)}, bf16[1,3584,1024]{2,1,0:T(8,128)(2,1)}, u32[]{:S(2)}) copy-start(bf16[1,3584,1024]{2,1,0:T(8,128)(2,1)} %param.10) | copy-start | bytes 22020100
  0.7 17.0 %copy-start.2 = (bf16[1,1024,3584]{2,1,0:T(8,128)(2,1)S(1)}, bf16[1,1024,3584]{2,1,0:T(8,128)(2,1)}, u32[]{:S(2)}) copy-start(bf16[1,1024,3584]{2,1,0:T(8,128)(2,1)} %param.11) | copy-start | bytes 22020100
  0.7 17.0 %copy-start.3 = (bf16[1,1,1,8]{3,2,1,0:T(2,128)(2,1)S(1)}, bf16[1,1,1,8]{3,2,1,0:T(2,128)(2,1)}, u32[]{:S(2)}) copy-start(bf16[1,1,1,8]{3,2,1,0:T(2,128)(2,1)} %param.7) | copy-start | bytes 52
  0.7 17.0 %copy-start.4 = (s32[1,1,1,8]{3,2,1,0:T(1,128)S(1)}, s32[1,1,1,8]{3,2,1,0:T(1,128)}, u32[]{:S(2)}) copy-start(s32[1,1,1,8]{3,2,1,0:T(1,128)} %param.8) | copy-start | bytes 100

commit v4 on v3

v4 whole, which is shorter than its diff:
```python
import functools

import jax
import jax.numpy as jnp
from jax import lax
from jax.experimental import pallas as pl
from jax.experimental.pallas import tpu as pltpu
from jax.sharding import PartitionSpec as P

LANES = 128
VMEM = pl.BlockSpec(memory_space=pltpu.VMEM)
HBM = pl.BlockSpec(memory_space=pltpu.HBM)


def block(total, rows):
    return next(
        size
        for size in range(total, 0, -LANES)
        if total % size == 0 and (size == LANES or rows * size <= 1 << 17)
    )


def matmul(x, y):
    return jnp.dot(x, y, preferred_element_type=jnp.float32)


def is_even(shape):
    return lax.rem(lax.broadcasted_iota(jnp.int32, shape, 0), 2) == 0


def parity():
    return lax.rem(lax.axis_index("ep"), 2)


def part_of(index, size):
    return pl.ds(pl.multiple_of(index * size, size), size)


def prepare_kernel(experts, tokens_hbm, weights_hbm, ids_hbm, sent_ref, tokens_ref, weights_ref, ids_ref, sems):
    copies = [
        pltpu.make_async_copy(source, target, sems.at[i])
        for i, (source, target) in enumerate(
            ((weights_hbm, weights_ref), (ids_hbm, ids_ref), (tokens_hbm, tokens_ref))
        )
    ]
    for copy in copies:
        copy.start()
    copies[0].wait()
    copies[1].wait()
    devices = sent_ref.shape[0]
    quarter = tokens_ref.shape[1] // 4
    shape = (2 * devices, LANES)
    expert = lax.rem(lax.div(lax.broadcasted_iota(jnp.int32, shape, 0), 2), experts)
    scale = jnp.zeros(shape, jnp.float32)
    for k in range(ids_ref.shape[1]):
        weight = weights_ref[:, k : k + 1].astype(jnp.float32)
        scale = scale + jnp.where(expert == ids_ref[:, k : k + 1], weight, 0.0)
    sent_ref[:, :, quarter:] = scale.astype(jnp.bfloat16).reshape(devices, 2, LANES)
    copies[2].wait()
    row = tokens_ref[...].astype(jnp.float32)
    quad = jnp.concatenate([row[:, i * quarter : (i + 1) * quarter] for i in range(4)], axis=0)
    quad = quad.astype(jnp.bfloat16)
    pairs = (quad[:2], quad[2:])

    @pl.loop(0, devices // 2)
    def _(i):
        for half in range(2):
            sent_ref[2 * i + half, :, :quarter] = pairs[half]


def project(rows, ref, half, columns):
    quarter = rows.shape[1]
    count = rows.shape[0]
    low = matmul(rows, ref[part_of(2 * half, quarter), columns])
    high = matmul(rows, ref[part_of(2 * half + 1, quarter), columns])
    return jnp.where(
        is_even(low.shape), low + pltpu.roll(high, count - 1, 0), high + pltpu.roll(low, 1, 0)
    )


def half_rows(ref):
    devices, _, size = ref.shape
    return ref[:, :, : size - LANES].reshape(2 * devices, size - LANES)


def scale_of(ref):
    devices, _, size = ref.shape
    scale = ref[:, :, size - LANES :].reshape(2 * devices, LANES)
    return scale[:, :1].astype(jnp.float32)


def first_kernel(own_ref, gate_ref, up_ref, gate_acc_ref, up_acc_ref):
    rows, half = half_rows(own_ref), parity()
    width = gate_ref.shape[1]
    step = block(width, rows.shape[0])

    @pl.loop(0, width // step)
    def _(i):
        columns = part_of(i, step)
        gate_acc_ref[:, columns] = project(rows, gate_ref, half, columns)
        up_acc_ref[:, columns] = project(rows, up_ref, half, columns)


def project_down(hidden_ref, down_ref, scale, half, store):
    hidden = hidden_ref[...]
    quarter = down_ref.shape[1] // 4
    step = block(quarter, hidden.shape[0])

    @pl.loop(0, quarter // step)
    def _(i):
        start = pl.multiple_of(2 * half * quarter + i * step, LANES)
        low = matmul(hidden, down_ref[:, pl.ds(start, step)])
        high = matmul(hidden, down_ref[:, pl.ds(start + quarter, step)])
        store(part_of(i, step), jnp.where(is_even(low.shape), low, high) * scale)


def second_kernel(
    own_ref, other_ref, gate_acc_ref, up_acc_ref, gate_ref, up_ref, down_ref, hidden_ref, out_ref
):
    rows, half = half_rows(other_ref), 1 - parity()
    width = gate_ref.shape[1]
    step = block(width, rows.shape[0])

    @pl.loop(0, width // step)
    def _(i):
        columns = part_of(i, step)
        gate = gate_acc_ref[:, columns] + project(rows, gate_ref, half, columns)
        up = up_acc_ref[:, columns] + project(rows, up_ref, half, columns)
        hidden_ref[:, columns] = (gate / (1.0 + jnp.exp(-gate)) * up).astype(jnp.bfloat16)

    scale = scale_of(own_ref)

    def store(columns, value):
        devices = out_ref.shape[0]
        out_ref[:, :, columns] = value.astype(jnp.bfloat16).reshape(devices, 2, value.shape[1])

    project_down(hidden_ref, down_ref, scale, half, store)


def third_kernel(hidden_ref, scale_ref, down_ref, out_ref):
    def store(columns, value):
        out_ref[:, columns] = value

    project_down(hidden_ref, down_ref, scale_of(scale_ref), parity(), store)


def add_kernel(kept_ref, received_ref, out_ref):
    devices, _, quarter = received_ref.shape
    received = received_ref[...].reshape(2 * devices, quarter).astype(jnp.float32)
    out_ref[...] = (kept_ref[...] + received).astype(jnp.bfloat16).reshape(devices, 2, quarter)


def mix_kernel(parts_ref, out_ref):
    devices, _, quarter = parts_ref.shape
    rows = parts_ref[...].reshape(2 * devices, quarter)
    shape = (16, 2 * devices)
    chosen = lax.rem(lax.broadcasted_iota(jnp.int32, shape, 1), 4) == lax.broadcasted_iota(
        jnp.int32, shape, 0
    )
    mixed = matmul(jnp.where(chosen, 1.0, 0.0).astype(jnp.bfloat16), rows)
    for i in range(4):
        out_ref[:, i * quarter : (i + 1) * quarter] = mixed[i : i + 1].astype(jnp.bfloat16)


def call(kernel, name, outs, ins, flops, scratch=(), in_specs=None):
    return pl.pallas_call(
        kernel,
        out_shape=outs,
        in_specs=in_specs or [VMEM] * len(ins),
        out_specs=jax.tree.map(lambda _: VMEM, outs),
        scratch_shapes=scratch,
        compiler_params=pltpu.CompilerParams(vmem_limit_bytes=24 << 20),
        cost_estimate=pl.CostEstimate(flops=flops, bytes_accessed=10**5, transcendentals=0),
        name=name,
    )(*ins)


def body(tokens, gate_weights, expert_ids, gate_proj, up_proj, down_proj):
    groups, experts = lax.axis_size("dp"), lax.axis_size("ep")
    devices = groups * experts
    features, width = tokens.shape[3], gate_proj.shape[2]
    top, quarter = expert_ids.shape[3], features // 4
    bf16, f32 = jnp.bfloat16, jnp.float32
    gate, up, down = gate_proj[0], up_proj[0], down_proj[0]
    swap = [(i, i ^ 1) for i in range(experts)]
    heavy = 2 * 10**10

    sent = call(
        functools.partial(prepare_kernel, experts),
        "prepare",
        jax.ShapeDtypeStruct((devices, 2, quarter + LANES), bf16),
        tuple(
            pltpu.with_memory_space_constraint(x[0, 0], pltpu.HBM)
            for x in (tokens, gate_weights, expert_ids)
        ),
        heavy,
        [
            pltpu.VMEM((1, features), bf16),
            pltpu.VMEM((1, top), bf16),
            pltpu.VMEM((1, top), jnp.int32),
            pltpu.SemaphoreType.DMA((3,)),
        ],
        [HBM] * 3,
    )
    own = lax.all_to_all(sent, ("dp", "ep"), 0, 0, tiled=True)
    other = lax.ppermute(own, "ep", swap)
    acc = jax.ShapeDtypeStruct((2 * devices, width), f32)
    gate_acc, up_acc = call(first_kernel, "first", (acc, acc), (own, gate, up), heavy)
    hidden, out = call(
        second_kernel,
        "second",
        (
            jax.ShapeDtypeStruct((2 * devices, width), bf16),
            jax.ShapeDtypeStruct((devices, 2, quarter), bf16),
        ),
        (own, other, gate_acc, up_acc, gate, up, down),
        heavy,
    )
    received = lax.ppermute(out, "ep", swap)
    kept = call(
        third_kernel,
        "third",
        jax.ShapeDtypeStruct((2 * devices, quarter), f32),
        (hidden, own, down),
        heavy,
    )
    summed = call(
        add_kernel, "add", jax.ShapeDtypeStruct((devices, 2, quarter), bf16), (kept, received), 10**6
    )
    parts = lax.all_to_all(summed, ("dp", "ep"), 0, 0, tiled=True)
    mixed = call(mix_kernel, "mix", jax.ShapeDtypeStruct((1, features), bf16), (parts,), 10**6)
    return mixed[None, None]


def solution(mesh):
    placed = (
        P("ep", "dp", None, None),
        P("ep", "dp", None, None),
        P("ep", "dp", None, None),
        P("ep", None, "dp"),
        P("ep", None, "dp"),
        P("ep", "dp", None),
    )
    return jax.shard_map(
        body, mesh=mesh, in_specs=placed, out_specs=P("ep", "dp", None, None), check_vma=False
    )
```

time: 34.7 us -> 32.5 us (0.937)
  blocking collectives: 28.6 us -> 25 us
  Pallas kernels: 5.07 us -> 6.23 us
  local copies, waits for them, and re-layouts: 0.73 us -> 0.02 us
  starting transfers between devices: 0 us -> 0.56 us
    all_to_all x2, blocking collectives: 28.6 us -> 25 us  [the longest x1 15.3 us: body(): own = lax.all_to_all(sent, ('dp', 'ep'), 0, 0, tiled=True)]
    pallas_call x3 -> x6, Pallas kernels: 5.07 us -> 6.23 us  [call(): pl.pallas_call(kernel, out_shape=outs, in_specs=in_specs or [VMEM] * len(...]
    unnamed x12 -> x8, local copies, waits for them, and re-layouts: 0.73 us -> 0.02 us
    ppermute x0 -> x2, starting transfers between devices: none -> 0.56 us  [the longest x1 0.3 us: body(): received = lax.ppermute(out, 'ep', swap)]
  transfers between devices with their start and end apart: 0 -> 2, of which waited for: 0 -> 1; matrix products, arithmetic and copies ran while one was open for 0% -> 0% of each run, Pallas kernels for 0% -> 7%
where the time goes in v4:
time: 32.5 us; the launch traced here: 32.3 us
  blocking collectives  25 us (77%)
  Pallas kernels  6.23 us (19%)
  starting transfers between devices  0.56 us (2%)
  waiting for transfers between devices  0.34 us (1%)
    all_to_all x1, blocking collectives, body(): own = lax.all_to_all(sent, ('dp', 'ep'), 0, 0, tiled=True)  15.3 us
    all_to_all x1, blocking collectives, body(): parts = lax.all_to_all(summed, ('dp', 'ep'), 0, 0, tiled=True)  9.69 us
    pallas_call x6, Pallas kernels, call(): pl.pallas_call(kernel, out_shape=outs, in_specs=in_specs or [VMEM] * len(...  6.23 us
  transfers between devices with their start and end apart: 2, of which 1 were waited for; matrix products, arithmetic and copies ran while one was open for 0% of the time, Pallas kernels for 7%

profile of v4, /device:TPU:0, one launch (start us, length us, event | category | flops | bytes accessed | tf_op | source)
XLA Modules:
  0.0 32.3 jit_solution(13177042531229067376)
XLA Ops:
  0.0 0.0 copy-start
  0.0 0.0 copy-start.1
  0.0 0.0 slice-start
  0.0 1.1 %prepare.1 = bf16[32,2,1024]{2,1,0:T(2,128)(2,1)S(1)} custom-call(bf16[1,3584]{1,0:T(2,128)(2,1)} %bitcast.15, bf16[1,8]{1,0:T(2,128)(2,1)} %bitcast.16, s32[1,8]{1,0:T(1,128)} %bitcast.17), custom_call_target="tpu_custom_call" | custom-call | flops 20000000000 | bytes 100000 | tf_op jit(solution)/shard_map/prepare/pallas_call | solution.py:166
  1.1 0.0 slice-start.1
  1.2 15.3 %all_to_all.10.own_ref.scale_ref = bf16[32,2,1024]{2,1,0:T(2,128)(2,1)S(1)} all-to-all(bf16[32,2,1024]{2,1,0:T(2,128)(2,1)S(1)} %prepare.1), channel_id=1, replica_groups=mesh['dp'=2,'ep'=16] {'dp','ep'}, dimensions={0} | all-to-all | bytes 262144 | tf_op jit(solution)/shard_map/all_to_all | solution.py:205
  16.5 0.3 collective-permute-start
  16.8 0.0 copy-done
  16.8 0.0 copy-done.1
  16.8 1.4 %first.1 = (f32[64,1024]{1,0:T(8,128)S(1)}, f32[64,1024]{1,0:T(8,128)S(1)}) custom-call(bf16[32,2,1024]{2,1,0:T(2,128)(2,1)S(1)} %all_to_all.10.own_ref.scale_ref, bf16[3584,1024]{1,0:T(8,128)(2,1)S(1)} %bitcast.7, bf16[3584,1024]{1,0:T(8,128)(2,1)S(1)} %bitcast.9), custom_call_target="tpu_custom_call" | custom-call | flops 20000000000 | bytes 100000 | tf_op jit(solution)/shard_map/first/pallas_call | solution.py:166
  18.2 0.0 collective-permute-done.other_ref
  18.2 0.0 slice-done
  18.2 0.0 slice-done.1
  18.2 2.1 %second.1 = (bf16[64,1024]{1,0:T(8,128)(2,1)S(1)}, bf16[32,2,896]{2,1,0:T(2,128)(2,1)S(1)}) custom-call(bf16[32,2,1024]{2,1,0:T(2,128)(2,1)S(1)} %all_to_all.10.own_ref.scale_ref, bf16[32,2,1024]{2,1,0:T(2,128)(2,1)S(1)} %collective-permute-done.other_ref, f32[64,1024]{1,0:T(8,128)S(1)} %get-tuple-element.9.gate_acc_ref, ...), custom_call_target="tpu_custom_call" | custom-call | flops 20000000000 | bytes 100000 | tf_op jit(solution)/shard_map/second/pallas_call | solution.py:166
  20.4 0.3 collective-permute-start.1
  20.7 0.7 %third.1.kept_ref = f32[64,896]{1,0:T(8,128)S(1)} custom-call(bf16[64,1024]{1,0:T(8,128)(2,1)S(1)} %get-tuple-element.11.hidden_ref, bf16[32,2,1024]{2,1,0:T(2,128)(2,1)S(1)} %all_to_all.10.own_ref.scale_ref, bf16[1024,3584]{1,0:T(8,128)(2,1)S(1)} %bitcast.14), custom_call_target="tpu_custom_call" | custom-call | flops 20000000000 | bytes 100000 | tf_op jit(solution)/shard_map/third/pallas_call | solution.py:166
  21.4 0.3 %collective-permute-done.1.received_ref = bf16[32,2,896]{2,1,0:T(2,128)(2,1)S(1)} collective-permute-done((bf16[32,2,896]{2,1,0:T(2,128)(2,1)S(1)}, bf16[32,2,896]{2,1,0:T(2,128)(2,1)S(1)}, u32[]{:S(2)}, u32[]{:S(2)}) %collective-permute-start.1) | collective-permute-done | bytes 114720 | tf_op jit(solution)/shard_map/ppermute | solution.py:219
  21.8 0.1 add.1
  21.8 9.7 %all_to_all.11.parts_ref = bf16[32,2,896]{2,1,0:T(2,128)(2,1)S(1)} all-to-all(bf16[32,2,896]{2,1,0:T(2,128)(2,1)S(1)} %add.1), channel_id=1, replica_groups=mesh['dp'=2,'ep'=16] {'dp','ep'}, dimensions={0} | all-to-all | bytes 229376 | tf_op jit(solution)/shard_map/all_to_all | solution.py:230
  31.5 0.7 %mix.1 = bf16[1,3584]{1,0:T(2,128)(2,1)} custom-call(bf16[32,2,896]{2,1,0:T(2,128)(2,1)S(1)} %all_to_all.11.parts_ref), custom_call_target="tpu_custom_call" | custom-call | flops 1000000 | bytes 100000 | tf_op jit(solution)/shard_map/mix/pallas_call | solution.py:166
  (1 shorter events, 0.0 us)
Async XLA Ops:
  0.0 16.8 %copy-start = (bf16[1,3584,1024]{2,1,0:T(8,128)(2,1)S(1)}, bf16[1,3584,1024]{2,1,0:T(8,128)(2,1)}, u32[]{:S(2)}) copy-start(bf16[1,3584,1024]{2,1,0:T(8,128)(2,1)} %param.9) | copy-start | bytes 22020100
  0.0 16.8 %copy-start.1 = (bf16[1,3584,1024]{2,1,0:T(8,128)(2,1)S(1)}, bf16[1,3584,1024]{2,1,0:T(8,128)(2,1)}, u32[]{:S(2)}) copy-start(bf16[1,3584,1024]{2,1,0:T(8,128)(2,1)} %param.10) | copy-start | bytes 22020100
  0.0 18.2 %slice-start = ((s8[7340032]{0:T(1024)(128)(4,1)}), s8[4194304]{0:T(1024)(128)(4,1)S(1)}, s32[]{:S(2)}) async-start(s8[7340032]{0:T(1024)(128)(4,1)} %bitcast.11), calls=%async_computation.2 | async-start | bytes 8388608
  1.1 17.1 %slice-start.1 = ((s8[7340032]{0:T(1024)(128)(4,1)}), s8[3145728]{0:T(1024)(128)(4,1)S(1)}, s32[]{:S(2)}) async-start(s8[7340032]{0:T(1024)(128)(4,1)} %bitcast.11), calls=%async_computation.3 | async-start | bytes 6291456
  16.5 1.7 %collective-permute-start = (bf16[32,2,1024]{2,1,0:T(2,128)(2,1)S(1)}, bf16[32,2,1024]{2,1,0:T(2,128)(2,1)S(1)}, u32[]{:S(2)}, u32[]{:S(2)}) collective-permute-start(bf16[32,2,1024]{2,1,0:T(2,128)(2,1)S(1)} %all_to_all.10.own_ref.scale_ref), channel_id=1, source_target_pairs={{0,1},{1,0},{2,3},{3,2},{4,5},{5,4},{6,7},{7,6},{8,9},{9,8},{10,11... | collective-permute-start | bytes 393224 | tf_op jit(solution)/shard_map/ppermute | solution.py:206
  20.4 1.4 %collective-permute-start.1 = (bf16[32,2,896]{2,1,0:T(2,128)(2,1)S(1)}, bf16[32,2,896]{2,1,0:T(2,128)(2,1)S(1)}, u32[]{:S(2)}, u32[]{:S(2)}) collective-permute-start(bf16[32,2,896]{2,1,0:T(2,128)(2,1)S(1)} %get-tuple-element.12), channel_id=1, source_target_pairs={{0,1},{1,0},{2,3},{3,2},{4,5},{5,4},{6,7},{7,6},{8,9},{9,8},{10,11... | collective-permute-start | bytes 344072 | tf_op jit(solution)/shard_map/ppermute | solution.py:219

commit v5 on v4

--- a/solution.py
+++ b/solution.py
@@ -20,8 +20,16 @@
     )
 
 
-def matmul(x, y):
-    return jnp.dot(x, y, preferred_element_type=jnp.float32)
+def matmul(x, ref, start, columns):
+    total = None
+    for k in range(0, x.shape[1], LANES):
+        part = jnp.dot(
+            x[:, k : k + LANES],
+            ref[pl.ds(pl.multiple_of(start + k, LANES), LANES), columns],
+            preferred_element_type=jnp.float32,
+        )
+        total = part if total is None else total + part
+    return total
 
 
 def is_even(shape):
@@ -51,10 +59,9 @@
     quarter = tokens_ref.shape[1] // 4
     shape = (2 * devices, LANES)
     expert = lax.rem(lax.div(lax.broadcasted_iota(jnp.int32, shape, 0), 2), experts)
-    scale = jnp.zeros(shape, jnp.float32)
-    for k in range(ids_ref.shape[1]):
-        weight = weights_ref[:, k : k + 1].astype(jnp.float32)
-        scale = scale + jnp.where(expert == ids_ref[:, k : k + 1], weight, 0.0)
+    expert = expert[:, : ids_ref.shape[1]]
+    chosen = jnp.where(expert == ids_ref[...], weights_ref[...].astype(jnp.float32), 0.0)
+    scale = jnp.broadcast_to(jnp.sum(chosen, axis=1, keepdims=True), shape)
     sent_ref[:, :, quarter:] = scale.astype(jnp.bfloat16).reshape(devices, 2, LANES)
     copies[2].wait()
     row = tokens_ref[...].astype(jnp.float32)
@@ -62,7 +69,7 @@
     quad = quad.astype(jnp.bfloat16)
     pairs = (quad[:2], quad[2:])
 
-    @pl.loop(0, devices // 2)
+    @pl.loop(0, devices // 2, unroll=min(16, devices // 2))
     def _(i):
         for half in range(2):
             sent_ref[2 * i + half, :, :quarter] = pairs[half]
@@ -71,8 +78,8 @@
 def project(rows, ref, half, columns):
     quarter = rows.shape[1]
     count = rows.shape[0]
-    low = matmul(rows, ref[part_of(2 * half, quarter), columns])
-    high = matmul(rows, ref[part_of(2 * half + 1, quarter), columns])
+    low = matmul(rows, ref, 2 * half * quarter, columns)
+    high = matmul(rows, ref, (2 * half + 1) * quarter, columns)
     return jnp.where(
         is_even(low.shape), low + pltpu.roll(high, count - 1, 0), high + pltpu.roll(low, 1, 0)
     )
@@ -106,11 +113,17 @@
     quarter = down_ref.shape[1] // 4
     step = block(quarter, hidden.shape[0])
 
+    if step == quarter:
+        both = matmul(hidden, down_ref, 0, part_of(half, 2 * quarter))
+        low, high = both[:, :quarter], both[:, quarter:]
+        store(slice(None), jnp.where(is_even(low.shape), low, high) * scale)
+        return
+
     @pl.loop(0, quarter // step)
     def _(i):
         start = pl.multiple_of(2 * half * quarter + i * step, LANES)
-        low = matmul(hidden, down_ref[:, pl.ds(start, step)])
-        high = matmul(hidden, down_ref[:, pl.ds(start + quarter, step)])
+        low = matmul(hidden, down_ref, 0, pl.ds(start, step))
+        high = matmul(hidden, down_ref, 0, pl.ds(start + quarter, step))
         store(part_of(i, step), jnp.where(is_even(low.shape), low, high) * scale)
 
 
@@ -152,14 +165,11 @@
 
 def mix_kernel(parts_ref, out_ref):
     devices, _, quarter = parts_ref.shape
-    rows = parts_ref[...].reshape(2 * devices, quarter)
-    shape = (16, 2 * devices)
-    chosen = lax.rem(lax.broadcasted_iota(jnp.int32, shape, 1), 4) == lax.broadcasted_iota(
-        jnp.int32, shape, 0
-    )
-    mixed = matmul(jnp.where(chosen, 1.0, 0.0).astype(jnp.bfloat16), rows)
+    rows = parts_ref[...].reshape(2 * devices, quarter).astype(jnp.float32)
+    mixed = jnp.sum(rows.reshape(devices // 4, 8, quarter), axis=0)
+    mixed = (mixed[:4] + mixed[4:]).astype(jnp.bfloat16)
     for i in range(4):
-        out_ref[:, i * quarter : (i + 1) * quarter] = mixed[i : i + 1].astype(jnp.bfloat16)
+        out_ref[:, i * quarter : (i + 1) * quarter] = mixed[i : i + 1]
 
 
 def call(kernel, name, outs, ins, flops, scratch=(), in_specs=None):

time: 32.5 us -> 31.6 us (0.972)
  Pallas kernels: 6.23 us -> 5.24 us
    pallas_call x6, Pallas kernels: 6.23 us -> 5.24 us  [call(): pl.pallas_call(kernel, out_shape=outs, in_specs=in_specs or [VMEM] * len(...]
  transfers between devices with their start and end apart: 2 -> 2, of which waited for: 1 -> 1; matrix products, arithmetic and copies ran while one was open for 0% -> 0% of each run, Pallas kernels for 7% -> 6%
where the time goes in v5:
time: 31.6 us; the launch traced here: 31.4 us
  blocking collectives  25 us (79%)
  Pallas kernels  5.24 us (17%)
  starting transfers between devices  0.54 us (2%)
  waiting for transfers between devices  0.47 us (1%)
    all_to_all x1, blocking collectives, body(): own = lax.all_to_all(sent, ('dp', 'ep'), 0, 0, tiled=True)  15.3 us
    all_to_all x1, blocking collectives, body(): parts = lax.all_to_all(summed, ('dp', 'ep'), 0, 0, tiled=True)  9.69 us
    pallas_call x6, Pallas kernels, call(): pl.pallas_call(kernel, out_shape=outs, in_specs=in_specs or [VMEM] * len(...  5.24 us
  transfers between devices with their start and end apart: 2, of which 1 were waited for; matrix products, arithmetic and copies ran while one was open for 0% of the time, Pallas kernels for 6%

profile of v5, /device:TPU:0, one launch (start us, length us, event | category | flops | bytes accessed | tf_op | source)
XLA Modules:
  0.0 31.4 jit_solution(10785766476916558406)
XLA Ops:
  0.0 0.0 copy-start
  0.0 0.0 copy-start.1
  0.0 0.0 slice-start
  0.0 1.0 %prepare.1 = bf16[32,2,1024]{2,1,0:T(2,128)(2,1)S(1)} custom-call(bf16[1,3584]{1,0:T(2,128)(2,1)} %bitcast.15, bf16[1,8]{1,0:T(2,128)(2,1)} %bitcast.16, s32[1,8]{1,0:T(1,128)} %bitcast.17), custom_call_target="tpu_custom_call" | custom-call | flops 20000000000 | bytes 100000 | tf_op jit(solution)/shard_map/prepare/pallas_call | solution.py:176
  1.0 0.0 slice-start.1
  1.0 15.3 %all_to_all.10.own_ref.scale_ref = bf16[32,2,1024]{2,1,0:T(2,128)(2,1)S(1)} all-to-all(bf16[32,2,1024]{2,1,0:T(2,128)(2,1)S(1)} %prepare.1), channel_id=1, replica_groups=mesh['dp'=2,'ep'=16] {'dp','ep'}, dimensions={0} | all-to-all | bytes 262144 | tf_op jit(solution)/shard_map/all_to_all | solution.py:215
  16.3 0.3 collective-permute-start
  16.6 0.0 copy-done
  16.6 0.0 copy-done.1
  16.6 1.1 %first.1 = (f32[64,1024]{1,0:T(8,128)S(1)}, f32[64,1024]{1,0:T(8,128)S(1)}) custom-call(bf16[32,2,1024]{2,1,0:T(2,128)(2,1)S(1)} %all_to_all.10.own_ref.scale_ref, bf16[3584,1024]{1,0:T(8,128)(2,1)S(1)} %bitcast.7, bf16[3584,1024]{1,0:T(8,128)(2,1)S(1)} %bitcast.9), custom_call_target="tpu_custom_call" | custom-call | flops 20000000000 | bytes 100000 | tf_op jit(solution)/shard_map/first/pallas_call | solution.py:176
  17.8 0.0 collective-permute-done.other_ref
  17.8 0.0 slice-done
  17.8 0.0 slice-done.1
  17.8 1.8 %second.1 = (bf16[64,1024]{1,0:T(8,128)(2,1)S(1)}, bf16[32,2,896]{2,1,0:T(2,128)(2,1)S(1)}) custom-call(bf16[32,2,1024]{2,1,0:T(2,128)(2,1)S(1)} %all_to_all.10.own_ref.scale_ref, bf16[32,2,1024]{2,1,0:T(2,128)(2,1)S(1)} %collective-permute-done.other_ref, f32[64,1024]{1,0:T(8,128)S(1)} %get-tuple-element.9.gate_acc_ref, ...), custom_call_target="tpu_custom_call" | custom-call | flops 20000000000 | bytes 100000 | tf_op jit(solution)/shard_map/second/pallas_call | solution.py:176
  19.6 0.3 collective-permute-start.1
  19.8 0.6 %third.1.kept_ref = f32[64,896]{1,0:T(8,128)S(1)} custom-call(bf16[64,1024]{1,0:T(8,128)(2,1)S(1)} %get-tuple-element.11.hidden_ref, bf16[32,2,1024]{2,1,0:T(2,128)(2,1)S(1)} %all_to_all.10.own_ref.scale_ref, bf16[1024,3584]{1,0:T(8,128)(2,1)S(1)} %bitcast.14), custom_call_target="tpu_custom_call" | custom-call | flops 20000000000 | bytes 100000 | tf_op jit(solution)/shard_map/third/pallas_call | solution.py:176
  20.5 0.5 %collective-permute-done.1.received_ref = bf16[32,2,896]{2,1,0:T(2,128)(2,1)S(1)} collective-permute-done((bf16[32,2,896]{2,1,0:T(2,128)(2,1)S(1)}, bf16[32,2,896]{2,1,0:T(2,128)(2,1)S(1)}, u32[]{:S(2)}, u32[]{:S(2)}) %collective-permute-start.1) | collective-permute-done | bytes 114720 | tf_op jit(solution)/shard_map/ppermute | solution.py:229
  21.0 0.1 add.1
  21.0 9.7 %all_to_all.11.parts_ref = bf16[32,2,896]{2,1,0:T(2,128)(2,1)S(1)} all-to-all(bf16[32,2,896]{2,1,0:T(2,128)(2,1)S(1)} %add.1), channel_id=1, replica_groups=mesh['dp'=2,'ep'=16] {'dp','ep'}, dimensions={0} | all-to-all | bytes 229376 | tf_op jit(solution)/shard_map/all_to_all | solution.py:240
  30.7 0.7 %mix.1 = bf16[1,3584]{1,0:T(2,128)(2,1)} custom-call(bf16[32,2,896]{2,1,0:T(2,128)(2,1)S(1)} %all_to_all.11.parts_ref), custom_call_target="tpu_custom_call" | custom-call | flops 1000000 | bytes 100000 | tf_op jit(solution)/shard_map/mix/pallas_call | solution.py:176
  (1 shorter events, 0.0 us)
Async XLA Ops:
  0.0 16.6 %copy-start = (bf16[1,3584,1024]{2,1,0:T(8,128)(2,1)S(1)}, bf16[1,3584,1024]{2,1,0:T(8,128)(2,1)}, u32[]{:S(2)}) copy-start(bf16[1,3584,1024]{2,1,0:T(8,128)(2,1)} %param.9) | copy-start | bytes 22020100
  0.0 16.6 %copy-start.1 = (bf16[1,3584,1024]{2,1,0:T(8,128)(2,1)S(1)}, bf16[1,3584,1024]{2,1,0:T(8,128)(2,1)}, u32[]{:S(2)}) copy-start(bf16[1,3584,1024]{2,1,0:T(8,128)(2,1)} %param.10) | copy-start | bytes 22020100
  0.0 17.8 %slice-start = ((s8[7340032]{0:T(1024)(128)(4,1)}), s8[4194304]{0:T(1024)(128)(4,1)S(1)}, s32[]{:S(2)}) async-start(s8[7340032]{0:T(1024)(128)(4,1)} %bitcast.11), calls=%async_computation.2 | async-start | bytes 8388608
  1.0 16.8 %slice-start.1 = ((s8[7340032]{0:T(1024)(128)(4,1)}), s8[3145728]{0:T(1024)(128)(4,1)S(1)}, s32[]{:S(2)}) async-start(s8[7340032]{0:T(1024)(128)(4,1)} %bitcast.11), calls=%async_computation.3 | async-start | bytes 6291456
  16.3 1.4 %collective-permute-start = (bf16[32,2,1024]{2,1,0:T(2,128)(2,1)S(1)}, bf16[32,2,1024]{2,1,0:T(2,128)(2,1)S(1)}, u32[]{:S(2)}, u32[]{:S(2)}) collective-permute-start(bf16[32,2,1024]{2,1,0:T(2,128)(2,1)S(1)} %all_to_all.10.own_ref.scale_ref), channel_id=1, source_target_pairs={{0,1},{1,0},{2,3},{3,2},{4,5},{5,4},{6,7},{7,6},{8,9},{9,8},{10,11... | collective-permute-start | bytes 393224 | tf_op jit(solution)/shard_map/ppermute | solution.py:216
  19.6 1.4 %collective-permute-start.1 = (bf16[32,2,896]{2,1,0:T(2,128)(2,1)S(1)}, bf16[32,2,896]{2,1,0:T(2,128)(2,1)S(1)}, u32[]{:S(2)}, u32[]{:S(2)}) collective-permute-start(bf16[32,2,896]{2,1,0:T(2,128)(2,1)S(1)} %get-tuple-element.12), channel_id=1, source_target_pairs={{0,1},{1,0},{2,3},{3,2},{4,5},{5,4},{6,7},{7,6},{8,9},{9,8},{10,11... | collective-permute-start | bytes 344072 | tf_op jit(solution)/shard_map/ppermute | solution.py:229

commit v6 on v5

--- a/solution.py
+++ b/solution.py
@@ -44,17 +44,19 @@
     return pl.ds(pl.multiple_of(index * size, size), size)
 
 
-def prepare_kernel(experts, tokens_hbm, weights_hbm, ids_hbm, sent_ref, tokens_ref, weights_ref, ids_ref, sems):
+def read_kernel(*refs):
+    sources, targets, sems = refs[:3], refs[3:6], refs[6]
     copies = [
         pltpu.make_async_copy(source, target, sems.at[i])
-        for i, (source, target) in enumerate(
-            ((weights_hbm, weights_ref), (ids_hbm, ids_ref), (tokens_hbm, tokens_ref))
-        )
+        for i, (source, target) in enumerate(zip(sources, targets))
     ]
     for copy in copies:
         copy.start()
-    copies[0].wait()
-    copies[1].wait()
+    for copy in copies:
+        copy.wait()
+
+
+def prepare_kernel(experts, tokens_ref, weights_ref, ids_ref, sent_ref):
     devices = sent_ref.shape[0]
     quarter = tokens_ref.shape[1] // 4
     shape = (2 * devices, LANES)
@@ -63,16 +65,11 @@
     chosen = jnp.where(expert == ids_ref[...], weights_ref[...].astype(jnp.float32), 0.0)
     scale = jnp.broadcast_to(jnp.sum(chosen, axis=1, keepdims=True), shape)
     sent_ref[:, :, quarter:] = scale.astype(jnp.bfloat16).reshape(devices, 2, LANES)
-    copies[2].wait()
     row = tokens_ref[...].astype(jnp.float32)
-    quad = jnp.concatenate([row[:, i * quarter : (i + 1) * quarter] for i in range(4)], axis=0)
-    quad = quad.astype(jnp.bfloat16)
-    pairs = (quad[:2], quad[2:])
-
-    @pl.loop(0, devices // 2, unroll=min(16, devices // 2))
-    def _(i):
-        for half in range(2):
-            sent_ref[2 * i + half, :, :quarter] = pairs[half]
+    quad = [row[:, i * quarter : (i + 1) * quarter] for i in range(4)]
+    pairs = jnp.concatenate(quad * 4, axis=0).astype(jnp.bfloat16).reshape(8, 2, quarter)
+    for i in range(0, devices, 8):
+        sent_ref[i : i + 8, :, :quarter] = pairs
 
 
 def project(rows, ref, half, columns):
@@ -195,22 +192,28 @@
     swap = [(i, i ^ 1) for i in range(experts)]
     heavy = 2 * 10**10
 
+    small = call(
+        read_kernel,
+        "read",
+        (
+            jax.ShapeDtypeStruct((1, features), bf16),
+            jax.ShapeDtypeStruct((1, top), bf16),
+            jax.ShapeDtypeStruct((1, top), jnp.int32),
+        ),
+        tuple(
+            pltpu.with_memory_space_constraint(x[0, 0], pltpu.HBM)
+            for x in (tokens, gate_weights, expert_ids)
+        ),
+        10**4,
+        [pltpu.SemaphoreType.DMA((3,))],
+        [HBM] * 3,
+    )
     sent = call(
         functools.partial(prepare_kernel, experts),
         "prepare",
         jax.ShapeDtypeStruct((devices, 2, quarter + LANES), bf16),
-        tuple(
-            pltpu.with_memory_space_constraint(x[0, 0], pltpu.HBM)
-            for x in (tokens, gate_weights, expert_ids)
-        ),
+        small,
         heavy,
-        [
-            pltpu.VMEM((1, features), bf16),
-            pltpu.VMEM((1, top), bf16),
-            pltpu.VMEM((1, top), jnp.int32),
-            pltpu.SemaphoreType.DMA((3,)),
-        ],
-        [HBM] * 3,
     )
     own = lax.all_to_all(sent, ("dp", "ep"), 0, 0, tiled=True)
     other = lax.ppermute(own, "ep", swap)

time: 31.6 us -> 31.5 us (level)
    pallas_call x6 -> x7, Pallas kernels: 5.24 us -> 5.12 us  [call(): pl.pallas_call(kernel, out_shape=outs, in_specs=in_specs or [VMEM] * len(...]
where the time goes in v6:
time: 31.5 us; the launch traced here: 31.3 us
  blocking collectives  25 us (79%)
  Pallas kernels  5.12 us (16%)
  starting transfers between devices  0.54 us (2%)
  waiting for transfers between devices  0.47 us (1%)
    all_to_all x1, blocking collectives, body(): own = lax.all_to_all(sent, ('dp', 'ep'), 0, 0, tiled=True)  15.3 us
    all_to_all x1, blocking collectives, body(): parts = lax.all_to_all(summed, ('dp', 'ep'), 0, 0, tiled=True)  9.69 us
    pallas_call x7, Pallas kernels, call(): pl.pallas_call(kernel, out_shape=outs, in_specs=in_specs or [VMEM] * len(...  5.12 us
  transfers between devices with their start and end apart: 2, of which 1 were waited for; matrix products, arithmetic and copies ran while one was open for 0% of the time, Pallas kernels for 6%

profile of v6, /device:TPU:0, one launch (start us, length us, event | category | flops | bytes accessed | tf_op | source)
XLA Modules:
  0.0 31.3 jit_solution(14591660999936910478)
XLA Ops:
  0.0 0.7 %read.1 = (bf16[1,3584]{1,0:T(2,128)(2,1)S(1)}, bf16[1,8]{1,0:T(2,128)(2,1)S(1)}, s32[1,8]{1,0:T(1,128)S(1)}) custom-call(bf16[1,3584]{1,0:T(2,128)(2,1)} %bitcast.15, bf16[1,8]{1,0:T(2,128)(2,1)} %bitcast.16, s32[1,8]{1,0:T(1,128)} %bitcast.17), custom_call_target="tpu_custom_call" | custom-call | flops 10000 | bytes 100000 | tf_op jit(solution)/shard_map/read/pallas_call | solution.py:173
  0.7 0.0 copy-start
  0.8 0.0 copy-start.1
  0.8 0.0 slice-start
  0.8 0.1 prepare.1
  0.9 0.0 slice-start.1
  0.9 15.3 %all_to_all.10.own_ref.scale_ref = bf16[32,2,1024]{2,1,0:T(2,128)(2,1)S(1)} all-to-all(bf16[32,2,1024]{2,1,0:T(2,128)(2,1)S(1)} %prepare.1), channel_id=1, replica_groups=mesh['dp'=2,'ep'=16] {'dp','ep'}, dimensions={0} | all-to-all | bytes 262144 | tf_op jit(solution)/shard_map/all_to_all | solution.py:218
  16.2 0.3 collective-permute-start
  16.5 0.0 copy-done
  16.5 0.0 copy-done.1
  16.5 1.2 %first.1 = (f32[64,1024]{1,0:T(8,128)S(1)}, f32[64,1024]{1,0:T(8,128)S(1)}) custom-call(bf16[32,2,1024]{2,1,0:T(2,128)(2,1)S(1)} %all_to_all.10.own_ref.scale_ref, bf16[3584,1024]{1,0:T(8,128)(2,1)S(1)} %bitcast.7, bf16[3584,1024]{1,0:T(8,128)(2,1)S(1)} %bitcast.9), custom_call_target="tpu_custom_call" | custom-call | flops 20000000000 | bytes 100000 | tf_op jit(solution)/shard_map/first/pallas_call | solution.py:173
  17.7 0.0 collective-permute-done.other_ref
  17.7 0.0 slice-done
  17.7 0.0 slice-done.1
  17.7 1.8 %second.1 = (bf16[64,1024]{1,0:T(8,128)(2,1)S(1)}, bf16[32,2,896]{2,1,0:T(2,128)(2,1)S(1)}) custom-call(bf16[32,2,1024]{2,1,0:T(2,128)(2,1)S(1)} %all_to_all.10.own_ref.scale_ref, bf16[32,2,1024]{2,1,0:T(2,128)(2,1)S(1)} %collective-permute-done.other_ref, f32[64,1024]{1,0:T(8,128)S(1)} %get-tuple-element.15.gate_acc_ref, ...), custom_call_target="tpu_custom_call" | custom-call | flops 20000000000 | bytes 100000 | tf_op jit(solution)/shard_map/second/pallas_call | solution.py:173
  19.5 0.3 collective-permute-start.1
  19.8 0.6 %third.1.kept_ref = f32[64,896]{1,0:T(8,128)S(1)} custom-call(bf16[64,1024]{1,0:T(8,128)(2,1)S(1)} %get-tuple-element.17.hidden_ref, bf16[32,2,1024]{2,1,0:T(2,128)(2,1)S(1)} %all_to_all.10.own_ref.scale_ref, bf16[1024,3584]{1,0:T(8,128)(2,1)S(1)} %bitcast.14), custom_call_target="tpu_custom_call" | custom-call | flops 20000000000 | bytes 100000 | tf_op jit(solution)/shard_map/third/pallas_call | solution.py:173
  20.4 0.5 %collective-permute-done.1.received_ref = bf16[32,2,896]{2,1,0:T(2,128)(2,1)S(1)} collective-permute-done((bf16[32,2,896]{2,1,0:T(2,128)(2,1)S(1)}, bf16[32,2,896]{2,1,0:T(2,128)(2,1)S(1)}, u32[]{:S(2)}, u32[]{:S(2)}) %collective-permute-start.1) | collective-permute-done | bytes 114720 | tf_op jit(solution)/shard_map/ppermute | solution.py:232
  20.9 0.1 add.1
  20.9 9.7 %all_to_all.11.parts_ref = bf16[32,2,896]{2,1,0:T(2,128)(2,1)S(1)} all-to-all(bf16[32,2,896]{2,1,0:T(2,128)(2,1)S(1)} %add.1), channel_id=1, replica_groups=mesh['dp'=2,'ep'=16] {'dp','ep'}, dimensions={0} | all-to-all | bytes 229376 | tf_op jit(solution)/shard_map/all_to_all | solution.py:243
  30.6 0.7 %mix.1 = bf16[1,3584]{1,0:T(2,128)(2,1)} custom-call(bf16[32,2,896]{2,1,0:T(2,128)(2,1)S(1)} %all_to_all.11.parts_ref), custom_call_target="tpu_custom_call" | custom-call | flops 1000000 | bytes 100000 | tf_op jit(solution)/shard_map/mix/pallas_call | solution.py:173
  (1 shorter events, 0.0 us)
Async XLA Ops:
  0.7 15.8 %copy-start = (bf16[1,3584,1024]{2,1,0:T(8,128)(2,1)S(1)}, bf16[1,3584,1024]{2,1,0:T(8,128)(2,1)}, u32[]{:S(2)}) copy-start(bf16[1,3584,1024]{2,1,0:T(8,128)(2,1)} %param.9) | copy-start | bytes 22020100
  0.8 15.8 %copy-start.1 = (bf16[1,3584,1024]{2,1,0:T(8,128)(2,1)S(1)}, bf16[1,3584,1024]{2,1,0:T(8,128)(2,1)}, u32[]{:S(2)}) copy-start(bf16[1,3584,1024]{2,1,0:T(8,128)(2,1)} %param.10) | copy-start | bytes 22020100
  0.8 16.9 %slice-start = ((s8[7340032]{0:T(1024)(128)(4,1)}), s8[4194304]{0:T(1024)(128)(4,1)S(1)}, s32[]{:S(2)}) async-start(s8[7340032]{0:T(1024)(128)(4,1)} %bitcast.11), calls=%async_computation.2 | async-start | bytes 8388608
  0.9 16.8 %slice-start.1 = ((s8[7340032]{0:T(1024)(128)(4,1)}), s8[3145728]{0:T(1024)(128)(4,1)S(1)}, s32[]{:S(2)}) async-start(s8[7340032]{0:T(1024)(128)(4,1)} %bitcast.11), calls=%async_computation.3 | async-start | bytes 6291456
  16.2 1.4 %collective-permute-start = (bf16[32,2,1024]{2,1,0:T(2,128)(2,1)S(1)}, bf16[32,2,1024]{2,1,0:T(2,128)(2,1)S(1)}, u32[]{:S(2)}, u32[]{:S(2)}) collective-permute-start(bf16[32,2,1024]{2,1,0:T(2,128)(2,1)S(1)} %all_to_all.10.own_ref.scale_ref), channel_id=1, source_target_pairs={{0,1},{1,0},{2,3},{3,2},{4,5},{5,4},{6,7},{7,6},{8,9},{9,8},{10,11... | collective-permute-start | bytes 393224 | tf_op jit(solution)/shard_map/ppermute | solution.py:219
  19.5 1.4 %collective-permute-start.1 = (bf16[32,2,896]{2,1,0:T(2,128)(2,1)S(1)}, bf16[32,2,896]{2,1,0:T(2,128)(2,1)S(1)}, u32[]{:S(2)}, u32[]{:S(2)}) collective-permute-start(bf16[32,2,896]{2,1,0:T(2,128)(2,1)S(1)} %get-tuple-element.18), channel_id=1, source_target_pairs={{0,1},{1,0},{2,3},{3,2},{4,5},{5,4},{6,7},{7,6},{8,9},{9,8},{10,11... | collective-permute-start | bytes 344072 | tf_op jit(solution)/shard_map/ppermute | solution.py:232

commit v7 on v6

--- a/solution.py
+++ b/solution.py
@@ -1,13 +1,17 @@
 import functools
+import math
 
 import jax
 import jax.numpy as jnp
 from jax import lax
 from jax.experimental import pallas as pl
 from jax.experimental.pallas import tpu as pltpu
+from jax.sharding import Mesh
 from jax.sharding import PartitionSpec as P
 
 LANES = 128
+NEAR = 4
+ORDER = ("near", "dp", "far")
 VMEM = pl.BlockSpec(memory_space=pltpu.VMEM)
 HBM = pl.BlockSpec(memory_space=pltpu.HBM)
 
@@ -37,7 +41,7 @@
 
 
 def parity():
-    return lax.rem(lax.axis_index("ep"), 2)
+    return lax.rem(lax.axis_index("near"), 2)
 
 
 def part_of(index, size):
@@ -56,20 +60,26 @@
         copy.wait()
 
 
-def prepare_kernel(experts, tokens_ref, weights_ref, ids_ref, sent_ref):
+def prepare_kernel(far, tokens_ref, weights_ref, ids_ref, sent_ref):
     devices = sent_ref.shape[0]
     quarter = tokens_ref.shape[1] // 4
-    shape = (2 * devices, LANES)
-    expert = lax.rem(lax.div(lax.broadcasted_iota(jnp.int32, shape, 0), 2), experts)
-    expert = expert[:, : ids_ref.shape[1]]
+    row_index = lax.broadcasted_iota(jnp.int32, (2 * devices, ids_ref.shape[1]), 0)
+    device = lax.div(row_index, 2)
+    expert = lax.rem(device, far) * NEAR + lax.div(device, devices // NEAR)
     chosen = jnp.where(expert == ids_ref[...], weights_ref[...].astype(jnp.float32), 0.0)
-    scale = jnp.broadcast_to(jnp.sum(chosen, axis=1, keepdims=True), shape)
+    scale = jnp.broadcast_to(jnp.sum(chosen, axis=1, keepdims=True), (2 * devices, LANES))
     sent_ref[:, :, quarter:] = scale.astype(jnp.bfloat16).reshape(devices, 2, LANES)
     row = tokens_ref[...].astype(jnp.float32)
     quad = [row[:, i * quarter : (i + 1) * quarter] for i in range(4)]
-    pairs = jnp.concatenate(quad * 4, axis=0).astype(jnp.bfloat16).reshape(8, 2, quarter)
-    for i in range(0, devices, 8):
-        sent_ref[i : i + 8, :, :quarter] = pairs
+    some = math.gcd(8, devices // NEAR)
+    pairs = [
+        jnp.concatenate(quad[2 * half : 2 * half + 2] * some, axis=0)
+        .astype(jnp.bfloat16)
+        .reshape(some, 2, quarter)
+        for half in range(2)
+    ]
+    for i in range(0, devices, some):
+        sent_ref[i : i + some, :, :quarter] = pairs[i // (devices // NEAR) % 2]
 
 
 def project(rows, ref, half, columns):
@@ -163,10 +173,15 @@
 def mix_kernel(parts_ref, out_ref):
     devices, _, quarter = parts_ref.shape
     rows = parts_ref[...].reshape(2 * devices, quarter).astype(jnp.float32)
-    mixed = jnp.sum(rows.reshape(devices // 4, 8, quarter), axis=0)
-    mixed = (mixed[:4] + mixed[4:]).astype(jnp.bfloat16)
-    for i in range(4):
-        out_ref[:, i * quarter : (i + 1) * quarter] = mixed[i : i + 1]
+    size = 2 * devices // NEAR
+    for half in range(2):
+        mine = sum(rows[i * size : (i + 1) * size] for i in range(half, NEAR, 2))
+        mine = jnp.sum(mine.reshape(size // 8, 8, quarter), axis=0)
+        mine = mine[:4] + mine[4:]
+        mine = (mine[:2] + mine[2:]).astype(jnp.bfloat16)
+        for i in range(2):
+            start = (2 * half + i) * quarter
+            out_ref[:, start : start + quarter] = mine[i : i + 1]
 
 
 def call(kernel, name, outs, ins, flops, scratch=(), in_specs=None):
@@ -183,13 +198,13 @@
 
 
 def body(tokens, gate_weights, expert_ids, gate_proj, up_proj, down_proj):
-    groups, experts = lax.axis_size("dp"), lax.axis_size("ep")
-    devices = groups * experts
+    far = lax.axis_size("far")
+    devices = lax.axis_size("dp") * far * NEAR
     features, width = tokens.shape[3], gate_proj.shape[2]
     top, quarter = expert_ids.shape[3], features // 4
     bf16, f32 = jnp.bfloat16, jnp.float32
     gate, up, down = gate_proj[0], up_proj[0], down_proj[0]
-    swap = [(i, i ^ 1) for i in range(experts)]
+    swap = [(i, i ^ 1) for i in range(NEAR)]
     heavy = 2 * 10**10
 
     small = call(
@@ -209,14 +224,14 @@
         [HBM] * 3,
     )
     sent = call(
-        functools.partial(prepare_kernel, experts),
+        functools.partial(prepare_kernel, far),
         "prepare",
         jax.ShapeDtypeStruct((devices, 2, quarter + LANES), bf16),
         small,
         heavy,
     )
-    own = lax.all_to_all(sent, ("dp", "ep"), 0, 0, tiled=True)
-    other = lax.ppermute(own, "ep", swap)
+    own = lax.all_to_all(sent, ORDER, 0, 0, tiled=True)
+    other = lax.ppermute(own, "near", swap)
     acc = jax.ShapeDtypeStruct((2 * devices, width), f32)
     gate_acc, up_acc = call(first_kernel, "first", (acc, acc), (own, gate, up), heavy)
     hidden, out = call(
@@ -229,7 +244,7 @@
         (own, other, gate_acc, up_acc, gate, up, down),
         heavy,
     )
-    received = lax.ppermute(out, "ep", swap)
+    received = lax.ppermute(out, "near", swap)
     kept = call(
         third_kernel,
         "third",
@@ -240,20 +255,24 @@
     summed = call(
         add_kernel, "add", jax.ShapeDtypeStruct((devices, 2, quarter), bf16), (kept, received), 10**6
     )
-    parts = lax.all_to_all(summed, ("dp", "ep"), 0, 0, tiled=True)
+    parts = lax.all_to_all(summed, ORDER, 0, 0, tiled=True)
     mixed = call(mix_kernel, "mix", jax.ShapeDtypeStruct((1, features), bf16), (parts,), 10**6)
     return mixed[None, None]
 
 
 def solution(mesh):
+    sizes = dict(mesh.shape)
+    devices = mesh.devices.reshape(sizes["dp"], sizes["ep"] // NEAR, NEAR)
+    split = Mesh(devices, ("dp", "far", "near"))
+    experts = ("far", "near")
     placed = (
-        P("ep", "dp", None, None),
-        P("ep", "dp", None, None),
-        P("ep", "dp", None, None),
-        P("ep", None, "dp"),
-        P("ep", None, "dp"),
-        P("ep", "dp", None),
+        P(experts, "dp", None, None),
+        P(experts, "dp", None, None),
+        P(experts, "dp", None, None),
+        P(experts, None, "dp"),
+        P(experts, None, "dp"),
+        P(experts, "dp", None),
     )
     return jax.shard_map(
-        body, mesh=mesh, in_specs=placed, out_specs=P("ep", "dp", None, None), check_vma=False
-    )
+        body, mesh=split, in_specs=placed, out_specs=P(experts, "dp", None, None), check_vma=False
+    )

time: 31.5 us -> 31.1 us (0.987)
    all_to_all x2, blocking collectives: 25 us -> 24.7 us  [the longest x1 14.9 us: body(): own = lax.all_to_all(sent, ORDER, 0, 0, tiled=True)]
  transfers between devices with their start and end apart: 2 -> 2, of which waited for: 1 -> 2; matrix products, arithmetic and copies ran while one was open for 0% -> 0% of each run, Pallas kernels for 6% -> 6%
where the time goes in v7:
time: 31.1 us; the launch traced here: 30.9 us
  blocking collectives  24.7 us (79%)
  Pallas kernels  5.12 us (16%)
  starting transfers between devices  0.5 us (2%)
  waiting for transfers between devices  0.43 us (1%)
    all_to_all x1, blocking collectives, body(): own = lax.all_to_all(sent, ORDER, 0, 0, tiled=True)  14.9 us
    all_to_all x1, blocking collectives, body(): parts = lax.all_to_all(summed, ORDER, 0, 0, tiled=True)  9.75 us
    pallas_call x7, Pallas kernels, call(): pl.pallas_call(kernel, out_shape=outs, in_specs=in_specs or [VMEM] * len(...  5.12 us
  transfers between devices with their start and end apart: 2, of which 2 were waited for; matrix products, arithmetic and copies ran while one was open for 0% of the time, Pallas kernels for 6%

profile of v7, /device:TPU:0, one launch (start us, length us, event | category | flops | bytes accessed | tf_op | source)
XLA Modules:
  0.0 30.9 jit_solution(11840269302124511225)
XLA Ops:
  0.0 0.7 %read.1 = (bf16[1,3584]{1,0:T(2,128)(2,1)S(1)}, bf16[1,8]{1,0:T(2,128)(2,1)S(1)}, s32[1,8]{1,0:T(1,128)S(1)}) custom-call(bf16[1,3584]{1,0:T(2,128)(2,1)} %bitcast.15, bf16[1,8]{1,0:T(2,128)(2,1)} %bitcast.16, s32[1,8]{1,0:T(1,128)} %bitcast.17), custom_call_target="tpu_custom_call" | custom-call | flops 10000 | bytes 100000 | tf_op jit(solution)/shard_map/read/pallas_call | solution.py:188
  0.7 0.0 copy-start
  0.8 0.0 copy-start.1
  0.8 0.0 slice-start
  0.8 0.1 prepare.1
  0.9 0.0 slice-start.1
  0.9 14.9 %all_to_all.10.own_ref.scale_ref = bf16[32,2,1024]{2,1,0:T(2,128)(2,1)S(1)} all-to-all(bf16[32,2,1024]{2,1,0:T(2,128)(2,1)S(1)} %prepare.1), channel_id=1, replica_groups=mesh['dp'=2,'far'=4,'near'=4] {'near','dp','far'}, dimensions={0} | all-to-all | bytes 262144 | tf_op jit(solution)/shard_map/all_to_all | solution.py:233
  15.9 0.1 collective-permute-start
  16.0 0.0 copy-done
  16.0 0.0 copy-done.1
  16.0 1.2 %first.1 = (f32[64,1024]{1,0:T(8,128)S(1)}, f32[64,1024]{1,0:T(8,128)S(1)}) custom-call(bf16[32,2,1024]{2,1,0:T(2,128)(2,1)S(1)} %all_to_all.10.own_ref.scale_ref, bf16[3584,1024]{1,0:T(8,128)(2,1)S(1)} %bitcast.7, bf16[3584,1024]{1,0:T(8,128)(2,1)S(1)} %bitcast.9), custom_call_target="tpu_custom_call" | custom-call | flops 20000000000 | bytes 100000 | tf_op jit(solution)/shard_map/first/pallas_call | solution.py:188
  17.1 0.1 collective-permute-done.other_ref
  17.2 0.0 slice-done
  17.2 0.0 slice-done.1
  17.2 1.8 %second.1 = (bf16[64,1024]{1,0:T(8,128)(2,1)S(1)}, bf16[32,2,896]{2,1,0:T(2,128)(2,1)S(1)}) custom-call(bf16[32,2,1024]{2,1,0:T(2,128)(2,1)S(1)} %all_to_all.10.own_ref.scale_ref, bf16[32,2,1024]{2,1,0:T(2,128)(2,1)S(1)} %collective-permute-done.other_ref, f32[64,1024]{1,0:T(8,128)S(1)} %get-tuple-element.15.gate_acc_ref, ...), custom_call_target="tpu_custom_call" | custom-call | flops 20000000000 | bytes 100000 | tf_op jit(solution)/shard_map/second/pallas_call | solution.py:188
  19.0 0.4 %collective-permute-start.1 = (bf16[32,2,896]{2,1,0:T(2,128)(2,1)S(1)}, bf16[32,2,896]{2,1,0:T(2,128)(2,1)S(1)}, u32[]{:S(2)}, u32[]{:S(2)}) collective-permute-start(bf16[32,2,896]{2,1,0:T(2,128)(2,1)S(1)} %get-tuple-element.18), channel_id=1, source_target_pairs={{0,1},{1,0},{2,3},{3,2},{4,5},{5,4},{6,7},{7,6},{8,9},{9,8},{10,11... | collective-permute-start | bytes 344072 | tf_op jit(solution)/shard_map/ppermute | solution.py:247
  19.4 0.6 %third.1.kept_ref = f32[64,896]{1,0:T(8,128)S(1)} custom-call(bf16[64,1024]{1,0:T(8,128)(2,1)S(1)} %get-tuple-element.17.hidden_ref, bf16[32,2,1024]{2,1,0:T(2,128)(2,1)S(1)} %all_to_all.10.own_ref.scale_ref, bf16[1024,3584]{1,0:T(8,128)(2,1)S(1)} %bitcast.14), custom_call_target="tpu_custom_call" | custom-call | flops 20000000000 | bytes 100000 | tf_op jit(solution)/shard_map/third/pallas_call | solution.py:188
  20.0 0.4 %collective-permute-done.1.received_ref = bf16[32,2,896]{2,1,0:T(2,128)(2,1)S(1)} collective-permute-done((bf16[32,2,896]{2,1,0:T(2,128)(2,1)S(1)}, bf16[32,2,896]{2,1,0:T(2,128)(2,1)S(1)}, u32[]{:S(2)}, u32[]{:S(2)}) %collective-permute-start.1) | collective-permute-done | bytes 114720 | tf_op jit(solution)/shard_map/ppermute | solution.py:247
  20.4 0.1 add.1
  20.4 9.8 %all_to_all.11.parts_ref = bf16[32,2,896]{2,1,0:T(2,128)(2,1)S(1)} all-to-all(bf16[32,2,896]{2,1,0:T(2,128)(2,1)S(1)} %add.1), channel_id=1, replica_groups=mesh['dp'=2,'far'=4,'near'=4] {'near','dp','far'}, dimensions={0} | all-to-all | bytes 229376 | tf_op jit(solution)/shard_map/all_to_all | solution.py:258
  30.2 0.6 %mix.1 = bf16[1,3584]{1,0:T(2,128)(2,1)} custom-call(bf16[32,2,896]{2,1,0:T(2,128)(2,1)S(1)} %all_to_all.11.parts_ref), custom_call_target="tpu_custom_call" | custom-call | flops 1000000 | bytes 100000 | tf_op jit(solution)/shard_map/mix/pallas_call | solution.py:188
  (1 shorter events, 0.0 us)
Async XLA Ops:
  0.7 15.2 %copy-start = (bf16[1,3584,1024]{2,1,0:T(8,128)(2,1)S(1)}, bf16[1,3584,1024]{2,1,0:T(8,128)(2,1)}, u32[]{:S(2)}) copy-start(bf16[1,3584,1024]{2,1,0:T(8,128)(2,1)} %param.9) | copy-start | bytes 22020100
  0.8 15.2 %copy-start.1 = (bf16[1,3584,1024]{2,1,0:T(8,128)(2,1)S(1)}, bf16[1,3584,1024]{2,1,0:T(8,128)(2,1)}, u32[]{:S(2)}) copy-start(bf16[1,3584,1024]{2,1,0:T(8,128)(2,1)} %param.10) | copy-start | bytes 22020100
  0.8 16.4 %slice-start = ((s8[7340032]{0:T(1024)(128)(4,1)}), s8[4194304]{0:T(1024)(128)(4,1)S(1)}, s32[]{:S(2)}) async-start(s8[7340032]{0:T(1024)(128)(4,1)} %bitcast.11), calls=%async_computation.2 | async-start | bytes 8388608
  0.9 16.3 %slice-start.1 = ((s8[7340032]{0:T(1024)(128)(4,1)}), s8[3145728]{0:T(1024)(128)(4,1)S(1)}, s32[]{:S(2)}) async-start(s8[7340032]{0:T(1024)(128)(4,1)} %bitcast.11), calls=%async_computation.3 | async-start | bytes 6291456
  15.9 1.3 %collective-permute-start = (bf16[32,2,1024]{2,1,0:T(2,128)(2,1)S(1)}, bf16[32,2,1024]{2,1,0:T(2,128)(2,1)S(1)}, u32[]{:S(2)}, u32[]{:S(2)}) collective-permute-start(bf16[32,2,1024]{2,1,0:T(2,128)(2,1)S(1)} %all_to_all.10.own_ref.scale_ref), channel_id=1, source_target_pairs={{0,1},{1,0},{2,3},{3,2},{4,5},{5,4},{6,7},{7,6},{8,9},{9,8},{10,11... | collective-permute-start | bytes 393224 | tf_op jit(solution)/shard_map/ppermute | solution.py:234
  19.0 1.4 %collective-permute-start.1 = (bf16[32,2,896]{2,1,0:T(2,128)(2,1)S(1)}, bf16[32,2,896]{2,1,0:T(2,128)(2,1)S(1)}, u32[]{:S(2)}, u32[]{:S(2)}) collective-permute-start(bf16[32,2,896]{2,1,0:T(2,128)(2,1)S(1)} %get-tuple-element.18), channel_id=1, source_target_pairs={{0,1},{1,0},{2,3},{3,2},{4,5},{5,4},{6,7},{7,6},{8,9},{9,8},{10,11... | collective-permute-start | bytes 344072 | tf_op jit(solution)/shard_map/ppermute | solution.py:247

commit v8 on v7

--- a/solution.py
+++ b/solution.py
@@ -139,9 +139,9 @@
 ):
     rows, half = half_rows(other_ref), 1 - parity()
     width = gate_ref.shape[1]
-    step = block(width, rows.shape[0])
-
-    @pl.loop(0, width // step)
+    step = min(512, block(width, rows.shape[0]))
+
+    @pl.loop(0, width // step, unroll=True)
     def _(i):
         columns = part_of(i, step)
         gate = gate_acc_ref[:, columns] + project(rows, gate_ref, half, columns)

time: 31.1 us -> 31 us (level)
  no operation moved by 1% of the time
where the time goes in v8:
time: 31 us; the launch traced here: 30.8 us
  blocking collectives  24.7 us (80%)
  Pallas kernels  5.05 us (16%)
  starting transfers between devices  0.48 us (2%)
  waiting for transfers between devices  0.45 us (1%)
    all_to_all x1, blocking collectives, body(): own = lax.all_to_all(sent, ORDER, 0, 0, tiled=True)  14.9 us
    all_to_all x1, blocking collectives, body(): parts = lax.all_to_all(summed, ORDER, 0, 0, tiled=True)  9.75 us
    pallas_call x7, Pallas kernels, call(): pl.pallas_call(kernel, out_shape=outs, in_specs=in_specs or [VMEM] * len(...  5.05 us
  transfers between devices with their start and end apart: 2, of which 2 were waited for; matrix products, arithmetic and copies ran while one was open for 0% of the time, Pallas kernels for 6%

profile of v8, /device:TPU:0, one launch (start us, length us, event | category | flops | bytes accessed | tf_op | source)
XLA Modules:
  0.0 30.8 jit_solution(9957768412426427109)
XLA Ops:
  0.0 0.7 %read.1 = (bf16[1,3584]{1,0:T(2,128)(2,1)S(1)}, bf16[1,8]{1,0:T(2,128)(2,1)S(1)}, s32[1,8]{1,0:T(1,128)S(1)}) custom-call(bf16[1,3584]{1,0:T(2,128)(2,1)} %bitcast.15, bf16[1,8]{1,0:T(2,128)(2,1)} %bitcast.16, s32[1,8]{1,0:T(1,128)} %bitcast.17), custom_call_target="tpu_custom_call" | custom-call | flops 10000 | bytes 100000 | tf_op jit(solution)/shard_map/read/pallas_call | solution.py:188
  0.7 0.0 copy-start
  0.8 0.0 copy-start.1
  0.8 0.0 slice-start
  0.8 0.1 prepare.1
  0.9 0.0 slice-start.1
  0.9 14.9 %all_to_all.10.own_ref.scale_ref = bf16[32,2,1024]{2,1,0:T(2,128)(2,1)S(1)} all-to-all(bf16[32,2,1024]{2,1,0:T(2,128)(2,1)S(1)} %prepare.1), channel_id=1, replica_groups=mesh['dp'=2,'far'=4,'near'=4] {'near','dp','far'}, dimensions={0} | all-to-all | bytes 262144 | tf_op jit(solution)/shard_map/all_to_all | solution.py:233
  15.9 0.1 collective-permute-start
  16.0 0.0 copy-done
  16.0 0.0 copy-done.1
  16.0 1.2 %first.1 = (f32[64,1024]{1,0:T(8,128)S(1)}, f32[64,1024]{1,0:T(8,128)S(1)}) custom-call(bf16[32,2,1024]{2,1,0:T(2,128)(2,1)S(1)} %all_to_all.10.own_ref.scale_ref, bf16[3584,1024]{1,0:T(8,128)(2,1)S(1)} %bitcast.7, bf16[3584,1024]{1,0:T(8,128)(2,1)S(1)} %bitcast.9), custom_call_target="tpu_custom_call" | custom-call | flops 20000000000 | bytes 100000 | tf_op jit(solution)/shard_map/first/pallas_call | solution.py:188
  17.1 0.1 collective-permute-done.other_ref
  17.2 0.0 slice-done
  17.2 0.0 slice-done.1
  17.2 1.7 %second.1 = (bf16[64,1024]{1,0:T(8,128)(2,1)S(1)}, bf16[32,2,896]{2,1,0:T(2,128)(2,1)S(1)}) custom-call(bf16[32,2,1024]{2,1,0:T(2,128)(2,1)S(1)} %all_to_all.10.own_ref.scale_ref, bf16[32,2,1024]{2,1,0:T(2,128)(2,1)S(1)} %collective-permute-done.other_ref, f32[64,1024]{1,0:T(8,128)S(1)} %get-tuple-element.15.gate_acc_ref, ...), custom_call_target="tpu_custom_call" | custom-call | flops 20000000000 | bytes 100000 | tf_op jit(solution)/shard_map/second/pallas_call | solution.py:188
  18.9 0.4 %collective-permute-start.1 = (bf16[32,2,896]{2,1,0:T(2,128)(2,1)S(1)}, bf16[32,2,896]{2,1,0:T(2,128)(2,1)S(1)}, u32[]{:S(2)}, u32[]{:S(2)}) collective-permute-start(bf16[32,2,896]{2,1,0:T(2,128)(2,1)S(1)} %get-tuple-element.18), channel_id=1, source_target_pairs={{0,1},{1,0},{2,3},{3,2},{4,5},{5,4},{6,7},{7,6},{8,9},{9,8},{10,11... | collective-permute-start | bytes 344072 | tf_op jit(solution)/shard_map/ppermute | solution.py:247
  19.3 0.6 %third.1.kept_ref = f32[64,896]{1,0:T(8,128)S(1)} custom-call(bf16[64,1024]{1,0:T(8,128)(2,1)S(1)} %get-tuple-element.17.hidden_ref, bf16[32,2,1024]{2,1,0:T(2,128)(2,1)S(1)} %all_to_all.10.own_ref.scale_ref, bf16[1024,3584]{1,0:T(8,128)(2,1)S(1)} %bitcast.14), custom_call_target="tpu_custom_call" | custom-call | flops 20000000000 | bytes 100000 | tf_op jit(solution)/shard_map/third/pallas_call | solution.py:188
  19.9 0.4 %collective-permute-done.1.received_ref = bf16[32,2,896]{2,1,0:T(2,128)(2,1)S(1)} collective-permute-done((bf16[32,2,896]{2,1,0:T(2,128)(2,1)S(1)}, bf16[32,2,896]{2,1,0:T(2,128)(2,1)S(1)}, u32[]{:S(2)}, u32[]{:S(2)}) %collective-permute-start.1) | collective-permute-done | bytes 114720 | tf_op jit(solution)/shard_map/ppermute | solution.py:247
  20.3 0.1 add.1
  20.4 9.8 %all_to_all.11.parts_ref = bf16[32,2,896]{2,1,0:T(2,128)(2,1)S(1)} all-to-all(bf16[32,2,896]{2,1,0:T(2,128)(2,1)S(1)} %add.1), channel_id=1, replica_groups=mesh['dp'=2,'far'=4,'near'=4] {'near','dp','far'}, dimensions={0} | all-to-all | bytes 229376 | tf_op jit(solution)/shard_map/all_to_all | solution.py:258
  30.1 0.6 %mix.1 = bf16[1,3584]{1,0:T(2,128)(2,1)} custom-call(bf16[32,2,896]{2,1,0:T(2,128)(2,1)S(1)} %all_to_all.11.parts_ref), custom_call_target="tpu_custom_call" | custom-call | flops 1000000 | bytes 100000 | tf_op jit(solution)/shard_map/mix/pallas_call | solution.py:188
  (1 shorter events, 0.0 us)
Async XLA Ops:
  0.7 15.2 %copy-start = (bf16[1,3584,1024]{2,1,0:T(8,128)(2,1)S(1)}, bf16[1,3584,1024]{2,1,0:T(8,128)(2,1)}, u32[]{:S(2)}) copy-start(bf16[1,3584,1024]{2,1,0:T(8,128)(2,1)} %param.9) | copy-start | bytes 22020100
  0.8 15.2 %copy-start.1 = (bf16[1,3584,1024]{2,1,0:T(8,128)(2,1)S(1)}, bf16[1,3584,1024]{2,1,0:T(8,128)(2,1)}, u32[]{:S(2)}) copy-start(bf16[1,3584,1024]{2,1,0:T(8,128)(2,1)} %param.10) | copy-start | bytes 22020100
  0.8 16.4 %slice-start = ((s8[7340032]{0:T(1024)(128)(4,1)}), s8[4194304]{0:T(1024)(128)(4,1)S(1)}, s32[]{:S(2)}) async-start(s8[7340032]{0:T(1024)(128)(4,1)} %bitcast.11), calls=%async_computation.2 | async-start | bytes 8388608
  0.9 16.3 %slice-start.1 = ((s8[7340032]{0:T(1024)(128)(4,1)}), s8[3145728]{0:T(1024)(128)(4,1)S(1)}, s32[]{:S(2)}) async-start(s8[7340032]{0:T(1024)(128)(4,1)} %bitcast.11), calls=%async_computation.3 | async-start | bytes 6291456
  15.9 1.3 %collective-permute-start = (bf16[32,2,1024]{2,1,0:T(2,128)(2,1)S(1)}, bf16[32,2,1024]{2,1,0:T(2,128)(2,1)S(1)}, u32[]{:S(2)}, u32[]{:S(2)}) collective-permute-start(bf16[32,2,1024]{2,1,0:T(2,128)(2,1)S(1)} %all_to_all.10.own_ref.scale_ref), channel_id=1, source_target_pairs={{0,1},{1,0},{2,3},{3,2},{4,5},{5,4},{6,7},{7,6},{8,9},{9,8},{10,11... | collective-permute-start | bytes 393224 | tf_op jit(solution)/shard_map/ppermute | solution.py:234
  18.9 1.4 %collective-permute-start.1 = (bf16[32,2,896]{2,1,0:T(2,128)(2,1)S(1)}, bf16[32,2,896]{2,1,0:T(2,128)(2,1)S(1)}, u32[]{:S(2)}, u32[]{:S(2)}) collective-permute-start(bf16[32,2,896]{2,1,0:T(2,128)(2,1)S(1)} %get-tuple-element.18), channel_id=1, source_target_pairs={{0,1},{1,0},{2,3},{3,2},{4,5},{5,4},{6,7},{7,6},{8,9},{9,8},{10,11... | collective-permute-start | bytes 344072 | tf_op jit(solution)/shard_map/ppermute | solution.py:247
